TPU v7x, 32 devices: a whole 2x2x4 slice. The times are simulated.
32 devices in a mesh: ez: 4 (over z), ey: 2 (over y), ex: 4 (over x, core).
Axes of the slice: x: 2, y: 2, z: 4, core: 2. Of those that a mesh axis runs over, the one named last changes fastest.
Arguments:
- tokens_in: bfloat16 [2, 8192, 1024], P(None, ('ez', 'ey', 'ex'))
- expert_ids: int32 [2, 2, 8192, 2], P(None, None, ('ez', 'ey', 'ex'))
- gate_vals: float32 [2, 2, 8192, 2], P(None, None, ('ez', 'ey', 'ex'))
- w_up1: bfloat16 [2, 32, 1024, 2816], P(None, ('ez', 'ey', 'ex'))
- w_up3: bfloat16 [2, 32, 1024, 2816], P(None, ('ez', 'ey', 'ex'))
- w_down: bfloat16 [2, 32, 2816, 1024], P(None, ('ez', 'ey', 'ex'))
Outputs:
- output: bfloat16 [2, 8192, 1024], P(None, ('ez', 'ey', 'ex'))
All inputs are finite; a program needn't handle non-finite values.
Results may differ from a plain program's by a relative error of at most 0.0151252.
Values are sent between devices in bfloat16 or wider.
A program may use at most 1 GiB of HBM per device.

v0:
```python
import jax
import jax.numpy as jnp
from jax import lax
from jax.sharding import PartitionSpec as P

ROUTE_SCALE = 2.5
MESH_AXES = ("ez", "ey", "ex")


def capacity_of(tok_mb, top_k, experts):
    return 2 * ((tok_mb * top_k + experts - 1) // experts)


def slot_layout(ids_blk, gates_blk, first_slot, num_slots, experts, capacity):
    chosen = (ids_blk[..., None] == jnp.arange(experts)).astype(jnp.int32)
    per_expert = jnp.sum(chosen, axis=-2)
    token_rank = jnp.cumsum(per_expert, axis=-2) - per_expert
    slot_pos = jnp.sum(chosen * token_rank[..., None, :], axis=-1)
    flat_slot = ids_blk * capacity + slot_pos - first_slot
    slot_match = flat_slot[..., None] == jnp.arange(num_slots)
    dispatch = jnp.any(slot_match, axis=-2).astype(jnp.bfloat16)
    combine = jnp.sum(jnp.where(slot_match, gates_blk[..., None], 0.0), axis=-2)
    return dispatch, combine


def expert_ffn(expert_rows, mat_up1, mat_up3, mat_down):
    gate_in = jnp.einsum("eldi,lig->eldg", expert_rows, mat_up1, preferred_element_type=jnp.float32)
    lin_in = jnp.einsum("eldi,lig->eldg", expert_rows, mat_up3, preferred_element_type=jnp.float32)
    hidden = (jax.nn.silu(gate_in) * lin_in).astype(jnp.bfloat16)
    return jnp.einsum("dkcf,kfh->dkch", hidden, mat_down, preferred_element_type=jnp.float32).astype(jnp.bfloat16)


def solution(mesh):
    n_dev = mesh.shape["ez"] * mesh.shape["ey"] * mesh.shape["ex"]
    tok_spec = P(None, MESH_AXES, None)
    route_spec = P(None, None, MESH_AXES, None)
    weight_spec = P(None, MESH_AXES, None, None)

    def device_body(tokens_in, expert_ids, gate_vals, w_up1, w_up3, w_down):
        n_layers, n_micro, tok_mb, top_k = expert_ids.shape
        exp_dev = w_up1.shape[1]
        hidden_size = tokens_in.shape[-1]
        experts = exp_dev * n_dev
        capacity = capacity_of(tok_mb, top_k, experts)
        batches = [tokens_in[mb_idx] for mb_idx in range(n_micro)]
        for layer_idx in range(n_layers):
            for mb_idx in range(n_micro):
                tokens = batches[mb_idx]
                dispatch, combine = slot_layout(expert_ids[layer_idx, mb_idx], gate_vals[layer_idx, mb_idx], 0, experts * capacity, experts, capacity)
                send_buf = jnp.einsum("tn,th->nh", dispatch, tokens, preferred_element_type=jnp.float32).astype(jnp.bfloat16)
                send_buf = send_buf.reshape(n_dev, exp_dev, capacity, hidden_size)
                recv_buf = lax.all_to_all(send_buf, MESH_AXES, 0, 0, tiled=True)
                expert_out = expert_ffn(recv_buf, w_up1[layer_idx], w_up3[layer_idx], w_down[layer_idx])
                returned = lax.all_to_all(expert_out, MESH_AXES, 0, 0, tiled=True)
                moe_sum = jnp.dot(combine, returned.reshape(experts * capacity, hidden_size), preferred_element_type=jnp.float32)
                batches[mb_idx] = (tokens.astype(jnp.float32) + ROUTE_SCALE * moe_sum).astype(jnp.bfloat16)
        return jnp.stack(batches)

    return jax.shard_map(device_body, mesh=mesh, in_specs=(tok_spec, route_spec, route_spec, weight_spec, weight_spec, weight_spec), out_specs=tok_spec, check_vma=False)
```

profile of v0, /device:TPU:0, one launch (start us, length us, event | category | flops | bytes accessed | tf_op | source)
XLA Modules:
  0.0 445.2 jit_solution(1119467001945940045)
XLA Ops:
  5.9 3.2 convolution_convert_fusion.3
  9.1 7.4 %all-to-all-start = ((bf16[32,1,32,1024]{3,2,1,0:T(8,128)(2,1)}), bf16[32,1,32,1024]{3,2,1,0:T(8,128)(2,1)S(1)}, u32[]{:S(2)}, u32[]{:S(2)}) async-start(bf16[32,1,32,1024]{3,2,1,0:T(8,128)(2,1)} %bitcast.6), calls=%async_computation | async-start | bytes 4194304 | tf_op jit(solution)/shard_map/all_to_all | solution.py:52
  16.4 2.1 convolution_convert_fusion.1
  18.5 46.6 %all-to-all-done = bf16[32,1,32,1024]{3,2,1,0:T(8,128)(2,1)S(1)} async-done(((bf16[32,1,32,1024]{3,2,1,0:T(8,128)(2,1)}), bf16[32,1,32,1024]{3,2,1,0:T(8,128)(2,1)S(1)}, u32[]{:S(2)}, u32[]{:S(2)}) %all-to-all-start) | async-done | bytes 2097184 | tf_op jit(solution)/shard_map/all_to_all | solution.py:52
  66.4 4.2 all-to-all-start.4
  70.6 12.0 %fusion.36 = f32[32,32,2816]{2,1,0:T(8,128)} fusion(bf16[2,1,1024,2816]{3,2,1,0:T(8,128)(2,1)} %param.9, bf16[32,1,32,1024]{3,2,1,0:T(8,128)(2,1)} %copy-done.3), kind=kOutput, calls=%fused_computation.48 | convolution fusion | flops 5905580032 | bytes 19398656 | tf_op jit(solution)/shard_map/eldi,lig->eldg/dot_general | solution.py:27
  82.6 21.7 %convert_bitcast_fusion.3 = bf16[32,1,32,1024]{3,2,1,0:T(8,128)(2,1)} fusion(bf16[2,1,2816,1024]{3,2,1,0:T(8,128)(2,1)} %param.11, f32[32,32,2816]{2,1,0:T(8,128)} %fusion.36, bf16[2,1,1024,2816]{3,2,1,0:T(8,128)(2,1)} %param.10, bf16[32,1,32,1024]{3,2,1,0:T(8,128)(2,1)} %copy-done.3), kind=kOutput, calls=%fused_computation.84 | convolution fusion | flops 11829510144 | bytes 27262976 | tf_op jit(solution)/shard_map/dkcf,kfh->dkch/dot_general | solution.py:30
  104.3 15.0 %all-to-all-done.4 = bf16[32,1,32,1024]{3,2,1,0:T(8,128)(2,1)S(1)} async-done(((bf16[32,1,32,1024]{3,2,1,0:T(8,128)(2,1)}), bf16[32,1,32,1024]{3,2,1,0:T(8,128)(2,1)S(1)}, u32[]{:S(2)}, u32[]{:S(2)}) %all-to-all-start.4) | async-done | bytes 2097184 | tf_op jit(solution)/shard_map/all_to_all | solution.py:52
  120.6 4.2 all-to-all-start.1
  124.7 12.2 %fusion.34 = f32[32,32,2816]{2,1,0:T(8,128)} fusion(bf16[2,1,1024,2816]{3,2,1,0:T(8,128)(2,1)} %param.9, bf16[32,1,32,1024]{3,2,1,0:T(8,128)(2,1)} %copy-done.1), kind=kOutput, calls=%fused_computation.46 | convolution fusion | flops 5905580032 | bytes 19398656 | tf_op jit(solution)/shard_map/eldi,lig->eldg/dot_general | solution.py:27
  136.9 21.6 %convert_bitcast_fusion.1 = bf16[32,1,32,1024]{3,2,1,0:T(8,128)(2,1)} fusion(bf16[2,1,2816,1024]{3,2,1,0:T(8,128)(2,1)} %param.11, f32[32,32,2816]{2,1,0:T(8,128)} %fusion.34, bf16[2,1,1024,2816]{3,2,1,0:T(8,128)(2,1)} %param.10, bf16[32,1,32,1024]{3,2,1,0:T(8,128)(2,1)} %copy-done.1), kind=kOutput, calls=%fused_computation.76 | convolution fusion | flops 11829510144 | bytes 27262976 | tf_op jit(solution)/shard_map/dkcf,kfh->dkch/dot_general | solution.py:30
  158.5 14.9 %all-to-all-done.1 = bf16[32,1,32,1024]{3,2,1,0:T(8,128)(2,1)S(1)} async-done(((bf16[32,1,32,1024]{3,2,1,0:T(8,128)(2,1)}), bf16[32,1,32,1024]{3,2,1,0:T(8,128)(2,1)S(1)}, u32[]{:S(2)}, u32[]{:S(2)}) %all-to-all-start.1) | async-done | bytes 2097184 | tf_op jit(solution)/shard_map/all_to_all | solution.py:54
  174.7 4.2 all-to-all-start.5
  179.5 2.3 fusion.87
  182.6 2.1 convolution_convert_fusion.2
  184.7 42.8 %all-to-all-done.5 = bf16[32,1,32,1024]{3,2,1,0:T(8,128)(2,1)S(1)} async-done(((bf16[32,1,32,1024]{3,2,1,0:T(8,128)(2,1)}), bf16[32,1,32,1024]{3,2,1,0:T(8,128)(2,1)S(1)}, u32[]{:S(2)}, u32[]{:S(2)}) %all-to-all-start.5) | async-done | bytes 2097184 | tf_op jit(solution)/shard_map/all_to_all | solution.py:54
  227.6 4.5 %all-to-all-start.2 = ((bf16[32,1,32,1024]{3,2,1,0:T(8,128)(2,1)}), bf16[32,1,32,1024]{3,2,1,0:T(8,128)(2,1)}, u32[]{:S(2)}, u32[]{:S(2)}) async-start(bf16[32,1,32,1024]{3,2,1,0:T(8,128)(2,1)} %bitcast.33), calls=%async_computation.2 | async-start | bytes 4194304 | tf_op jit(solution)/shard_map/all_to_all | solution.py:52
  234.1 2.0 convolution_convert_fusion
  236.2 44.7 %all-to-all-done.2 = bf16[32,1,32,1024]{3,2,1,0:T(8,128)(2,1)} async-done(((bf16[32,1,32,1024]{3,2,1,0:T(8,128)(2,1)}), bf16[32,1,32,1024]{3,2,1,0:T(8,128)(2,1)}, u32[]{:S(2)}, u32[]{:S(2)}) %all-to-all-start.2) | async-done | bytes 2097184 | tf_op jit(solution)/shard_map/all_to_all | solution.py:52
  280.9 3.9 all-to-all-start.6
  284.8 11.8 %fusion.25 = f32[32,32,2816]{2,1,0:T(8,128)} fusion(bf16[2,1,1024,2816]{3,2,1,0:T(8,128)(2,1)} %param.9, bf16[32,1,32,1024]{3,2,1,0:T(8,128)(2,1)} %all-to-all-done.2), kind=kOutput, calls=%fused_computation.37 | convolution fusion | flops 5905580032 | bytes 19398656 | tf_op jit(solution)/shard_map/eldi,lig->eldg/dot_general | solution.py:27
  296.6 21.8 %convert_bitcast_fusion.2 = bf16[32,1,32,1024]{3,2,1,0:T(8,128)(2,1)} fusion(bf16[2,1,2816,1024]{3,2,1,0:T(8,128)(2,1)} %param.11, f32[32,32,2816]{2,1,0:T(8,128)} %fusion.25, bf16[2,1,1024,2816]{3,2,1,0:T(8,128)(2,1)} %param.10, bf16[32,1,32,1024]{3,2,1,0:T(8,128)(2,1)} %all-to-all-done.2), kind=kOutput, calls=%fused_computation.80 | convolution fusion | flops 11829510144 | bytes 27262976 | tf_op jit(solution)/shard_map/dkcf,kfh->dkch/dot_general | solution.py:30
  318.4 15.0 %all-to-all-done.6 = bf16[32,1,32,1024]{3,2,1,0:T(8,128)(2,1)S(1)} async-done(((bf16[32,1,32,1024]{3,2,1,0:T(8,128)(2,1)}), bf16[32,1,32,1024]{3,2,1,0:T(8,128)(2,1)S(1)}, u32[]{:S(2)}, u32[]{:S(2)}) %all-to-all-start.6) | async-done | bytes 2097184 | tf_op jit(solution)/shard_map/all_to_all | solution.py:52
  334.8 4.2 all-to-all-start.3
  338.9 12.0 %fusion.23 = f32[32,32,2816]{2,1,0:T(8,128)} fusion(bf16[2,1,1024,2816]{3,2,1,0:T(8,128)(2,1)} %param.9, bf16[32,1,32,1024]{3,2,1,0:T(8,128)(2,1)} %copy-done.2), kind=kOutput, calls=%fused_computation.35 | convolution fusion | flops 5905580032 | bytes 19398656 | tf_op jit(solution)/shard_map/eldi,lig->eldg/dot_general | solution.py:27
  351.0 21.7 %convert_bitcast_fusion = bf16[32,1,32,1024]{3,2,1,0:T(8,128)(2,1)} fusion(bf16[2,1,2816,1024]{3,2,1,0:T(8,128)(2,1)} %param.11, f32[32,32,2816]{2,1,0:T(8,128)} %fusion.23, bf16[2,1,1024,2816]{3,2,1,0:T(8,128)(2,1)} %param.10, bf16[32,1,32,1024]{3,2,1,0:T(8,128)(2,1)} %copy-done.2), kind=kOutput, calls=%fused_computation.72 | convolution fusion | flops 11829510144 | bytes 27262976 | tf_op jit(solution)/shard_map/dkcf,kfh->dkch/dot_general | solution.py:30
  372.7 14.9 %all-to-all-done.3 = bf16[32,1,32,1024]{3,2,1,0:T(8,128)(2,1)S(1)} async-done(((bf16[32,1,32,1024]{3,2,1,0:T(8,128)(2,1)}), bf16[32,1,32,1024]{3,2,1,0:T(8,128)(2,1)S(1)}, u32[]{:S(2)}, u32[]{:S(2)}) %all-to-all-start.3) | async-done | bytes 2097184 | tf_op jit(solution)/shard_map/all_to_all | solution.py:54
  387.6 4.3 all-to-all-start.7
  392.5 1.5 fusion.88
  394.0 46.4 %all-to-all-done.7 = bf16[32,1,32,1024]{3,2,1,0:T(8,128)(2,1)} async-done(((bf16[32,1,32,1024]{3,2,1,0:T(8,128)(2,1)}), bf16[32,1,32,1024]{3,2,1,0:T(8,128)(2,1)}, u32[]{:S(2)}, u32[]{:S(2)}) %all-to-all-start.7) | async-done | bytes 2097184 | tf_op jit(solution)/shard_map/all_to_all | solution.py:54
  440.4 2.4 fusion.89
  442.8 2.1 pad_maximum_fusion
  (60 shorter events, 15.0 us)
Async XLA Ops:
  0.0 16.4 %copy-start.4 = (bf16[2,256,1024]{2,1,0:T(8,128)(2,1)S(1)}, bf16[2,256,1024]{2,1,0:T(8,128)(2,1)}, u32[]{:S(2)}) copy-start(bf16[2,256,1024]{2,1,0:T(8,128)(2,1)} %param.6) | copy-start | bytes 3145732
  9.1 56.0 %all-to-all-start = ((bf16[32,1,32,1024]{3,2,1,0:T(8,128)(2,1)}), bf16[32,1,32,1024]{3,2,1,0:T(8,128)(2,1)S(1)}, u32[]{:S(2)}, u32[]{:S(2)}) async-start(bf16[32,1,32,1024]{3,2,1,0:T(8,128)(2,1)} %bitcast.6), calls=%async_computation | async-start | bytes 4194304 | tf_op jit(solution)/shard_map/all_to_all | solution.py:52
  65.1 1.3 copy-start.3
  66.4 52.8 %all-to-all-start.4 = ((bf16[32,1,32,1024]{3,2,1,0:T(8,128)(2,1)}), bf16[32,1,32,1024]{3,2,1,0:T(8,128)(2,1)S(1)}, u32[]{:S(2)}, u32[]{:S(2)}) async-start(bf16[32,1,32,1024]{3,2,1,0:T(8,128)(2,1)} %bitcast.62), calls=%async_computation.4 | async-start | bytes 4194304 | tf_op jit(solution)/shard_map/all_to_all | solution.py:52
  119.2 1.3 copy-start.1
  120.6 52.8 %all-to-all-start.1 = ((bf16[32,1,32,1024]{3,2,1,0:T(8,128)(2,1)}), bf16[32,1,32,1024]{3,2,1,0:T(8,128)(2,1)S(1)}, u32[]{:S(2)}, u32[]{:S(2)}) async-start(bf16[32,1,32,1024]{3,2,1,0:T(8,128)(2,1)} %convert_bitcast_fusion.3), calls=%async_computation.1 | async-start | bytes 4194304 | tf_op jit(solution)/shard_map/all_to_all | solution.py:54
  136.9 42.3 %copy-start.8 = (f32[2,2,256,2]{2,3,1,0:T(2,128)S(1)}, f32[2,2,256,2]{2,3,1,0:T(2,128)}, u32[]{:S(2)}) copy-start(f32[2,2,256,2]{2,3,1,0:T(2,128)} %param.8) | copy-start | bytes 24580
  173.4 1.4 copy-start
  174.7 52.8 %all-to-all-start.5 = ((bf16[32,1,32,1024]{3,2,1,0:T(8,128)(2,1)}), bf16[32,1,32,1024]{3,2,1,0:T(8,128)(2,1)S(1)}, u32[]{:S(2)}, u32[]{:S(2)}) async-start(bf16[32,1,32,1024]{3,2,1,0:T(8,128)(2,1)} %convert_bitcast_fusion.1), calls=%async_computation.5 | async-start | bytes 4194304 | tf_op jit(solution)/shard_map/all_to_all | solution.py:54
  181.8 0.8 copy-start.5
  227.6 53.3 %all-to-all-start.2 = ((bf16[32,1,32,1024]{3,2,1,0:T(8,128)(2,1)}), bf16[32,1,32,1024]{3,2,1,0:T(8,128)(2,1)}, u32[]{:S(2)}, u32[]{:S(2)}) async-start(bf16[32,1,32,1024]{3,2,1,0:T(8,128)(2,1)} %bitcast.33), calls=%async_computation.2 | async-start | bytes 4194304 | tf_op jit(solution)/shard_map/all_to_all | solution.py:52
  233.3 0.8 copy-start.7
  280.9 52.5 %all-to-all-start.6 = ((bf16[32,1,32,1024]{3,2,1,0:T(8,128)(2,1)}), bf16[32,1,32,1024]{3,2,1,0:T(8,128)(2,1)S(1)}, u32[]{:S(2)}, u32[]{:S(2)}) async-start(bf16[32,1,32,1024]{3,2,1,0:T(8,128)(2,1)} %bitcast.86), calls=%async_computation.6 | async-start | bytes 4194304 | tf_op jit(solution)/shard_map/all_to_all | solution.py:52
  333.4 1.3 copy-start.2
  334.8 52.8 %all-to-all-start.3 = ((bf16[32,1,32,1024]{3,2,1,0:T(8,128)(2,1)}), bf16[32,1,32,1024]{3,2,1,0:T(8,128)(2,1)S(1)}, u32[]{:S(2)}, u32[]{:S(2)}) async-start(bf16[32,1,32,1024]{3,2,1,0:T(8,128)(2,1)} %convert_bitcast_fusion.2), calls=%async_computation.3 | async-start | bytes 4194304 | tf_op jit(solution)/shard_map/all_to_all | solution.py:54
  350.9 41.5 %copy-start.6 = (bf16[256,1024]{1,0:T(8,128)(2,1)S(1)}, bf16[256,1024]{1,0:T(8,128)(2,1)}, u32[]{:S(2)}) copy-start(bf16[256,1024]{1,0:T(8,128)(2,1)} %copy-done.5) | copy-start | bytes 1572868
  387.6 52.8 %all-to-all-start.7 = ((bf16[32,1,32,1024]{3,2,1,0:T(8,128)(2,1)}), bf16[32,1,32,1024]{3,2,1,0:T(8,128)(2,1)}, u32[]{:S(2)}, u32[]{:S(2)}) async-start(bf16[32,1,32,1024]{3,2,1,0:T(8,128)(2,1)} %convert_bitcast_fusion), calls=%async_computation.7 | async-start | bytes 4194304 | tf_op jit(solution)/shard_map/all_to_all | solution.py:54
where the time goes:
time: 451 us; the launch traced here: 445 us
  waiting for transfers between devices  240 us (53%)
  matrix products  151 us (33%)
  starting transfers between devices  36.7 us (8%)
  local copies, waits for them, and re-layouts  8.49 us (2%)
  other arithmetic  7.93 us (2%)
    all_to_all x4, waiting for transfers between devices, device_body(): recv_buf = lax.all_to_all(send_buf, MESH_AXES, 0, 0, tiled=True)  121 us
    all_to_all x4, waiting for transfers between devices, device_body(): returned = lax.all_to_all(expert_out, MESH_AXES, 0, 0, tiled=True)  119 us
    dot_general x4, matrix products, expert_ffn(): jnp.einsum('dkcf,kfh->dkch', hidden, mat_down, preferred_element_type=jnp...  86.8 us
    dot_general x4, matrix products, expert_ffn(): jnp.einsum('eldi,lig->eldg', expert_rows, mat_up1, preferred_element_type...  48 us
    all_to_all x4, starting transfers between devices, device_body(): recv_buf = lax.all_to_all(send_buf, MESH_AXES, 0, 0, tiled=True)  19.9 us
    all_to_all x4, starting transfers between devices, device_body(): returned = lax.all_to_all(expert_out, MESH_AXES, 0, 0, tiled=True)  16.8 us
    dot_general x4, matrix products, device_body(): jnp.einsum('tn,th->nh', dispatch, tokens, preferred_element_type=jnp.floa...  9.37 us
  transfers between devices with their start and end apart: 8, of which 8 were waited for; matrix products, arithmetic and copies ran while one was open for 33% of the time, Pallas kernels for 0%

commit v1 on v0

v1 whole, which is shorter than its diff:
```python
import functools

import jax
import jax.numpy as jnp
from jax import lax
from jax.experimental import pallas as pl
from jax.experimental.pallas import tpu as pltpu
from jax.sharding import PartitionSpec as P

ROUTE_SCALE = 2.5
MESH_AXES = ("ez", "ey", "ex")
NZ, NC = 4, 8
TILE = 256
BF16, F32 = jnp.bfloat16, jnp.float32
MESH = pl.DeviceIdType.MESH


def dot(lhs, rhs):
    return jnp.dot(lhs, rhs, preferred_element_type=F32)


def dot_t(lhs, rhs):
    return lax.dot_general(lhs, rhs, (((0,), (0,)), ((), ())), preferred_element_type=F32)


def moe_kernel(rows, tok_ref, grow_ref, prow_ref, gate_ref, w1_hbm, w3_hbm, wd_hbm, out_ref,
               ucur, tsend, trecv, ssend, xrecv, osend, rrecv, ysend, yrecv, w1, w3, wd, hid,
               w_sem, tz_s, tz_r, sp_s, sp_r, op_s, op_r, yz_s, yz_r):
    n_layers, n_mb = grow_ref.shape[0], grow_ref.shape[1]
    slots, width = NC * 32, ucur.shape[-1]
    ffn = w1.shape[-1]
    me_z = lax.axis_index("ez")
    me_c = lax.axis_index("ey") * 4 + lax.axis_index("ex")

    def peer_z(k):
        return 2 * ((me_z // 2 + k // 2) % 2) + (me_z % 2 + k % 2) % 2

    def peer_c(d):
        return (me_c + d) % NC

    def w_copies(layer):
        return [pltpu.make_async_copy(src.at[layer, 0], dst, w_sem.at[i])
                for i, (src, dst) in enumerate(((w1_hbm, w1), (w3_hbm, w3), (wd_hbm, wd)))]

    def t_copy(mb, k):
        return pltpu.make_async_remote_copy(
            src_ref=tsend.at[mb, k], dst_ref=trecv.at[mb, k], send_sem=tz_s.at[mb, k], recv_sem=tz_r.at[mb, k],
            device_id={"ez": peer_z(k)}, device_id_type=MESH)

    def y_copy(mb, k):
        return pltpu.make_async_remote_copy(
            src_ref=ysend.at[mb, k], dst_ref=yrecv.at[mb, me_z], send_sem=yz_s.at[mb, k], recv_sem=yz_r.at[mb, me_z],
            device_id={"ez": peer_z(k)}, device_id_type=MESH)

    def y_wait(mb, k):
        src = peer_z(k)
        pltpu.make_async_remote_copy(
            src_ref=ysend.at[mb, k], dst_ref=yrecv.at[mb, src], send_sem=yz_s.at[mb, k], recv_sem=yz_r.at[mb, src],
            device_id={"ez": src}, device_id_type=MESH).wait_recv()

    def plane_copy(src, dst, s_sem, r_sem, mb, k, d):
        c = peer_c(d)
        return pltpu.make_async_remote_copy(
            src_ref=src.at[mb, k, c], dst_ref=dst.at[mb, k, me_c], send_sem=s_sem.at[mb, k], recv_sem=r_sem.at[mb, k],
            device_id={"ey": c // 4, "ex": c % 4}, device_id_type=MESH)

    def plane_all(src, dst, s_sem, r_sem, mb, k):
        part = pl.ds(0, NC - 1)
        return pltpu.make_async_remote_copy(
            src_ref=src.at[mb, k, part], dst_ref=dst.at[mb, k, part], send_sem=s_sem.at[mb, k],
            recv_sem=r_sem.at[mb, k], device_id={"ey": peer_c(1) // 4, "ex": peer_c(1) % 4}, device_id_type=MESH)

    def one_hot(cond):
        return jnp.where(cond, 1.0, 0.0).astype(BF16)

    def send_tokens(layer, mb):
        g0 = grow_ref[layer, mb, 0:1, :]
        g1 = grow_ref[layer, mb, 1:2, :]
        tok = ucur[mb]
        for k in (1, 2, 3, 0):
            base = peer_z(k) * rows
            row = lax.broadcasted_iota(jnp.int32, (rows, tok.shape[0]), 0) + base
            packed = dot(one_hot((row == g0) | (row == g1)), tok).astype(BF16)
            if k == 0:
                trecv[mb, 0] = packed
            else:
                tsend[mb, k] = packed
                t_copy(mb, k).start()

    def expand_matrix(layer, mb, k):
        row = lax.broadcasted_iota(jnp.int32, (rows, slots), 0)
        return one_hot(row == prow_ref[layer, mb, k:k + 1, :])

    def expand(layer, mb, k):
        if k:
            t_copy(mb, k).wait_recv()
        ssend[mb, k] = dot_t(expand_matrix(layer, mb, k), trecv[mb, k]).astype(BF16).reshape(NC, 32, width)
        for d in range(1, NC):
            plane_copy(ssend, xrecv, sp_s, sp_r, mb, k, d).start()
        xrecv[mb, k, me_c] = ssend[mb, k, me_c]

    def expert(mb, k):
        plane_all(ssend, xrecv, sp_s, sp_r, mb, k).wait_recv()

        def up(t, _):
            cols = pl.ds(pl.multiple_of(t * TILE, TILE), TILE)
            x = xrecv[mb, k].reshape(slots, width)
            a = dot(x, w1[:, cols])
            b = dot(x, w3[:, cols])
            hid[:, cols] = (jax.nn.silu(a) * b).astype(BF16)
            return 0

        lax.fori_loop(0, ffn // TILE, up, 0)

        def down(t, _):
            cols = pl.ds(pl.multiple_of(t * TILE, TILE), TILE)
            osend[mb, k, :, :, cols] = dot(hid[...], wd[:, cols]).astype(BF16).reshape(NC, 32, TILE)
            return 0

        lax.fori_loop(0, width // TILE, down, 0)
        for d in range(1, NC):
            plane_copy(osend, rrecv, op_s, op_r, mb, k, d).start()
        rrecv[mb, k, me_c] = osend[mb, k, me_c]

    def give_back(layer, mb, k):
        plane_all(osend, rrecv, op_s, op_r, mb, k).wait_recv()
        packed = dot(expand_matrix(layer, mb, k), rrecv[mb, k].reshape(slots, width)).astype(BF16)
        if k == 0:
            yrecv[mb, me_z] = packed
        else:
            ysend[mb, k] = packed
            y_copy(mb, k).start()

    def combine(layer, mb):
        for k in (1, 2, 3):
            y_wait(mb, k)
        y = yrecv[mb].reshape(NZ * rows, width)
        row = lax.broadcasted_iota(jnp.int32, (NZ * rows, ucur.shape[1]), 0)
        total = jnp.zeros(ucur.shape[1:], F32)
        for j in range(2):
            picked = dot_t(one_hot(row == grow_ref[layer, mb, j:j + 1, :]), y)
            total = total + gate_ref[layer, :, 2 * mb + j:2 * mb + j + 1] * picked
        ucur[mb] = (ucur[mb].astype(F32) + ROUTE_SCALE * total).astype(BF16)
        for k in range(NZ):
            if k:
                t_copy(mb, k).wait_send()
                y_copy(mb, k).wait_send()
            plane_all(ssend, xrecv, sp_s, sp_r, mb, k).wait_send()
            plane_all(osend, rrecv, op_s, op_r, mb, k).wait_send()

    for copy in w_copies(0):
        copy.start()
    ucur[...] = tok_ref[...]
    barrier = pltpu.get_barrier_semaphore()
    for k in range(1, NZ):
        pl.semaphore_signal(barrier, inc=1, device_id={"ez": peer_z(k)}, device_id_type=MESH)
    for d in range(1, NC):
        c = peer_c(d)
        pl.semaphore_signal(barrier, inc=1, device_id={"ey": c // 4, "ex": c % 4}, device_id_type=MESH)
    pl.semaphore_wait(barrier, NZ - 1 + NC - 1)

    send_tokens(0, 0)
    send_tokens(0, 1)

    def layer_step(layer, _):
        expand(layer, 0, 0)
        expand(layer, 1, 0)
        for copy in w_copies(layer):
            copy.wait()
        expert(0, 0)
        expand(layer, 0, 1)
        expert(1, 0)
        give_back(layer, 0, 0)
        expert(0, 1)
        expand(layer, 0, 2)
        give_back(layer, 0, 1)
        expert(0, 2)
        expand(layer, 0, 3)
        give_back(layer, 0, 2)
        expert(0, 3)
        give_back(layer, 1, 0)
        expand(layer, 1, 1)
        give_back(layer, 0, 3)
        expert(1, 1)
        expand(layer, 1, 2)
        give_back(layer, 1, 1)
        expert(1, 2)
        expand(layer, 1, 3)
        give_back(layer, 1, 2)
        expert(1, 3)

        @pl.when(layer + 1 < n_layers)
        def _():
            for copy in w_copies(layer + 1):
                copy.start()

        give_back(layer, 1, 3)
        for mb in range(n_mb):
            combine(layer, mb)

            @pl.when(layer + 1 < n_layers)
            def _():
                send_tokens(layer + 1, mb)
        return 0

    lax.fori_loop(0, n_layers, layer_step, 0)
    out_ref[...] = ucur[...]


def run_moe(rows, collective_id, tokens, grow, prow, gates, w_up1, w_up3, w_down):
    n_mb, n_tok, width = tokens.shape
    ffn = w_up1.shape[-1]
    vmem = pl.BlockSpec(memory_space=pltpu.VMEM)
    hbm = pl.BlockSpec(memory_space=pl.ANY)
    packed = pltpu.VMEM((n_mb, NZ, rows, width), BF16)
    padded = pltpu.VMEM((n_mb, NZ, NC, 32, width), BF16)
    pair = pltpu.SemaphoreType.DMA((n_mb, NZ))
    return pl.pallas_call(
        functools.partial(moe_kernel, rows),
        out_shape=jax.ShapeDtypeStruct(tokens.shape, BF16),
        in_specs=[vmem] * 4 + [hbm] * 3,
        out_specs=vmem,
        scratch_shapes=[
            pltpu.VMEM((n_mb, n_tok, width), BF16),
            packed, packed, padded, padded, padded, padded, packed, packed,
            pltpu.VMEM((width, ffn), BF16), pltpu.VMEM((width, ffn), BF16), pltpu.VMEM((ffn, width), BF16),
            pltpu.VMEM((NC * 32, ffn), BF16),
            pltpu.SemaphoreType.DMA((3,)),
        ] + [pair] * 8,
        compiler_params=pltpu.CompilerParams(
            collective_id=collective_id, has_side_effects=True, vmem_limit_bytes=67_000_000),
        name=f"moe_rows_{rows}",
    )(tokens, grow, prow, gates, w_up1, w_up3, w_down)


def solution(mesh):
    tok_spec = P(None, MESH_AXES, None)
    route_spec = P(None, None, MESH_AXES, None)
    weight_spec = P(None, MESH_AXES, None, None)

    def device_body(tokens_in, expert_ids, gate_vals, w_up1, w_up3, w_down):
        n_layers, n_mb, n_tok, top_k = expert_ids.shape
        experts = NZ * NC
        me_z = lax.axis_index("ez")
        me_c = lax.axis_index("ey") * 4 + lax.axis_index("ex")
        chosen = (expert_ids[..., None] == jnp.arange(experts)).astype(F32)
        per_tok = jnp.sum(chosen, axis=3)
        before = (jnp.arange(n_tok)[:, None] > jnp.arange(n_tok)[None, :]).astype(BF16)
        rank_e = jnp.einsum("ts,lmse->lmte", before, per_tok.astype(BF16), preferred_element_type=F32)
        counts = jnp.sum(per_tok, axis=2).astype(jnp.int32)
        by_plane = counts.reshape(n_layers, n_mb, NZ, NC)
        off_e = (jnp.cumsum(by_plane, axis=-1) - by_plane).reshape(n_layers, n_mb, experts)
        in_plane = jnp.sum(chosen * (rank_e + off_e[:, :, None, :].astype(F32))[:, :, :, None, :], axis=-1)
        in_plane = in_plane.astype(jnp.int32)
        plane = expert_ids // NC

        all_counts = lax.all_gather(by_plane, MESH_AXES)
        fits = jnp.max(jnp.sum(all_counts, axis=-1)) <= 176
        all_counts = all_counts.reshape(NZ, NC, n_layers, n_mb, NZ, NC)
        mine = lax.dynamic_index_in_dim(all_counts, me_c, 1, keepdims=False)
        mine = lax.dynamic_index_in_dim(mine, me_z, 3, keepdims=False)
        order = [2 * ((me_z // 2 + k // 2) % 2) + (me_z % 2 + k % 2) % 2 for k in range(NZ)]
        mine = jnp.stack([lax.dynamic_index_in_dim(mine, zs, 0, keepdims=False) for zs in order], axis=2)
        start = jnp.cumsum(mine, axis=-1) - mine
        lane = jnp.arange(32)
        prow = jnp.where(lane < mine[..., None], start[..., None] + lane, -1).reshape(n_layers, n_mb, NZ, NC * 32)
        gates = gate_vals.transpose(0, 2, 1, 3).reshape(n_layers, n_tok, n_mb * top_k)

        def branch(rows, collective_id):
            def run():
                grow = (plane * rows + in_plane).transpose(0, 1, 3, 2)
                return run_moe(rows, collective_id, tokens_in, grow, prow, gates, w_up1, w_up3, w_down)
            return run

        return lax.cond(fits, branch(176, 1), branch(256, 2))

    return jax.shard_map(device_body, mesh=mesh, in_specs=(tok_spec, route_spec, route_spec, weight_spec, weight_spec, weight_spec), out_specs=tok_spec, check_vma=False)
```

time: 451 us -> 385 us (0.85)
  Pallas kernels: 0 us -> 319 us
  waiting for transfers between devices: 240 us -> 0 us
  matrix products: 151 us -> 0.2 us
  blocking collectives: 0 us -> 44 us
  starting transfers between devices: 36.7 us -> 0 us
    pallas_call x0 -> x1, Pallas kernels: none -> 319 us  [run_moe(): pl.pallas_call(functools.partial(moe_kernel, rows), out_shape=jax.ShapeDt...]
    all_to_all x8 -> x0, waiting for transfers between devices: 240 us -> none  [the longest x4 121 us: device_body(): recv_buf = lax.all_to_all(send_buf, MESH_AXES, 0, 0, tiled=True)]
    dot_general x16 -> x1, matrix products: 151 us -> 0.2 us  [device_body(): jnp.einsum('ts,lmse->lmte', before, per_tok.astype(BF16), preferred_eleme...]
    all_gather x0 -> x1, blocking collectives: none -> 44 us  [device_body(): all_counts = lax.all_gather(by_plane, MESH_AXES)]
    all_to_all x8 -> x0, starting transfers between devices: 36.7 us -> none  [the longest x4 19.9 us: device_body(): recv_buf = lax.all_to_all(send_buf, MESH_AXES, 0, 0, tiled=True)]
  transfers between devices with their start and end apart: 8 -> 0, of which waited for: 8 -> 0; matrix products, arithmetic and copies ran while one was open for 33% -> 0% of each run, Pallas kernels for 0% -> 0%
where the time goes in v1:
time: 385 us; the launch traced here: 379 us
  Pallas kernels  319 us (83%)
  blocking collectives  44 us (11%)
  other arithmetic  10.1 us (3%)
  local copies, waits for them, and re-layouts  4.53 us (1%)
    pallas_call x1, Pallas kernels, run_moe(): pl.pallas_call(functools.partial(moe_kernel, rows), out_shape=jax.ShapeDt...  319 us
    all_gather x1, blocking collectives, device_body(): all_counts = lax.all_gather(by_plane, MESH_AXES)  44 us

profile of v1, /device:TPU:0, one launch (start us, length us, event | category | flops | bytes accessed | tf_op | source)
XLA Modules:
  0.0 379.0 jit_solution(4621611493158073036)
XLA Ops:
  0.0 0.7 broadcast_compare_fusion
  0.7 0.1 lt.82
  0.8 0.7 copy.100
  1.5 0.7 broadcast_and_fusion
  2.2 0.8 convert_reduce_fusion
  3.0 0.1 convert_element_type.48
  3.1 0.7 reduce_window_sum.19
  3.8 0.1 reduce_window_sum.20
  3.9 0.1 convert_element_type.45
  4.0 0.2 fusion.8
  4.2 0.8 select_reduce_fusion
  5.0 44.0 %all_gather.3 = s32[32,2,2,4,8]{4,3,2,1,0:T(4,128)S(1)} all-gather(s32[1,2,2,4,8]{4,3,2,1,0:T(4,128)S(1)} %convert_element_type.45), channel_id=1, replica_groups=mesh['ez'=4,'ey'=2,'ex'=4] {'ez','ey','ex'}, dimensions={0}, use_global_device_ids=true | all-gather | bytes 16896 | tf_op jit(solution)/shard_map/all_gather | solution.py:257
  49.0 1.4 reduce_window_sum.21
  50.4 2.3 reduce_sum.37
  52.8 0.7 reduce_max.9
  54.2 322.6 %conditional.1 = (bf16[2,256,1024]{2,1,0:T(8,128)(2,1)}) conditional(s32[]{:T(128)} %convert_element_type.46, (s32[2,2,256,2]{2,3,1,0:T(2,128)}, s32[2,2,256,2]{2,3,1,0:T(2,128)S(1)}, bf16[2,256,1024]{2,1,0:T(8,128)(2,1)}, s32[2,2,4,256]{3,2,1,0:T(4,128)S(1)}, f32[2,256,2,2]{1,0,3,2:T(2,128)S(1)}, ...), branch_computations={%region_7.8_spmd.clone, %region_8.9_spmd.clone} | conditional | flops 32896 | bytes 250900 | solution.py:275
  54.4 1.3 fusion.7.grow_ref
  55.7 0.1 lt.108
  55.8 0.1 lt.107
  55.9 0.1 add.167
  56.0 0.1 add.166
  56.1 0.6 add_select_fusion.1.prow_ref
  56.7 0.9 copy.76.gate_ref
  57.5 319.2 %moe_rows_176.1 = bf16[2,256,1024]{2,1,0:T(8,128)(2,1)} custom-call(bf16[2,256,1024]{2,1,0:T(8,128)(2,1)} %get-tuple-element.183.tok_ref, s32[2,2,2,256]{3,2,1,0:T(2,128)} %fusion.7.grow_ref, s32[2,2,4,256]{3,2,1,0:T(4,128)} %add_select_fusion.1.prow_ref, f32[2,256,4]{2,1,0:T(8,128)} %copy.76.gate_ref, bf16[2,1,1024,2816]{3,2,1,0:T(8,128)(2,1)} %get-tuple-element.187.w1_hbm, ...), custom_call_target="tpu_custom_call" | custom-call | tf_op jit(solution)/shard_map/cond/branch_1_fun/moe_rows_176/pallas_call | solution.py:218
  376.7 2.3 copy.104
  (9 shorter events, 0.1 us)

commit v2 on v1

v2 whole, which is shorter than its diff:
```python
import functools

import jax
import jax.numpy as jnp
from jax import lax
from jax.experimental import pallas as pl
from jax.experimental.pallas import tpu as pltpu
from jax.sharding import PartitionSpec as P

ROUTE_SCALE = 2.5
MESH_AXES = ("ez", "ey", "ex")
NZ, NC, CAP = 4, 8, 32
EXPERTS, SLOTS = NZ * NC, NC * CAP
TILE = 256
BF16, F32 = jnp.bfloat16, jnp.float32
MESH = pl.DeviceIdType.MESH


def dot(lhs, rhs):
    return jnp.dot(lhs, rhs, preferred_element_type=F32)


def dot_t(lhs, rhs):
    return lax.dot_general(lhs, rhs, (((0,), (0,)), ((), ())), preferred_element_type=F32)


def dot_nt(lhs, rhs):
    return lax.dot_general(lhs, rhs, (((1,), (1,)), ((), ())), preferred_element_type=F32)


def one_hot(cond):
    return jnp.where(cond, 1.0, 0.0).astype(BF16)


def iota(shape, dim):
    return lax.broadcasted_iota(jnp.int32, shape, dim)


def place():
    return lax.axis_index("ez"), lax.axis_index("ey") * 4 + lax.axis_index("ex")


def peer_of(me_z, k):
    return 2 * ((me_z // 2 + k // 2) % 2) + (me_z % 2 + k % 2) % 2


def plane_id(c):
    return {"ey": c // 4, "ex": c % 4}


def route_kernel(ids_ref, meta_ref, prow_ref, peak_ref, mine, seen, s_sem, r_sem):
    n_layers, n_mb, n_tok, top_k = ids_ref.shape
    lanes = n_layers * n_mb * EXPERTS
    me_z, me_c = place()
    me = me_z * NC + me_c
    n_dev = NZ * NC

    def target(d):
        dev = (me + d) % n_dev
        return {"ez": dev // NC, "ey": dev % NC // 4, "ex": dev % 4}

    barrier = pltpu.get_barrier_semaphore()

    def greet(d, _):
        pl.semaphore_signal(barrier, inc=1, device_id=target(d), device_id_type=MESH)
        return 0

    lax.fori_loop(1, n_dev, greet, 0)

    lane = iota((n_tok, lanes), 1)
    chosen = []
    for j in range(top_k):
        ids = jnp.zeros((n_tok, lanes), jnp.int32)
        for layer in range(n_layers):
            for mb in range(n_mb):
                ids = jnp.where(lane // EXPERTS == layer * n_mb + mb, ids_ref[layer, mb, :, j:j + 1], ids)
        chosen.append(jnp.where(ids == lane % EXPERTS, 1.0, 0.0))
    per_tok = (chosen[0] + chosen[1]).astype(BF16)
    counts = dot(jnp.ones((8, n_tok), BF16), per_tok)
    mine[...] = counts
    seen[me] = counts
    pl.semaphore_wait(barrier, n_dev - 1)

    def share(d, _):
        pltpu.make_async_remote_copy(src_ref=mine, dst_ref=seen.at[me], send_sem=s_sem, recv_sem=r_sem,
                                     device_id=target(d), device_id_type=MESH).start()
        return 0

    lax.fori_loop(1, n_dev, share, 0)

    before = one_hot(iota((n_tok, n_tok), 0) > iota((n_tok, n_tok), 1))
    rank = dot(before, per_tok)
    row, col = iota((lanes, lanes), 0), iota((lanes, lanes), 1)
    same_plane = row // NC == col // NC
    start = dot(counts.astype(BF16), one_hot(same_plane & (row < col)))[0:1]
    pick = one_hot(iota((8, lanes), 0) == iota((8, lanes), 1) // EXPERTS)
    for j in range(top_k):
        base = dot_nt(pick, (chosen[j] * (lane % EXPERTS // NC).astype(F32)).astype(BF16)) * SLOTS
        packed = base + dot_nt(pick, (chosen[j] * (rank + start)).astype(BF16))
        padded = base + dot_nt(pick, (chosen[j] * (rank + (lane % NC * CAP).astype(F32))).astype(BF16))
        for layer in range(n_layers):
            for mb in range(n_mb):
                i = layer * n_mb + mb
                meta_ref[layer, mb, j:j + 1, :] = packed[i:i + 1].astype(jnp.int32)
                meta_ref[layer, mb, top_k + j:top_k + j + 1, :] = padded[i:i + 1].astype(jnp.int32)

    rest = pltpu.make_async_remote_copy(
        src_ref=seen.at[pl.ds(0, n_dev - 1)], dst_ref=seen.at[pl.ds(0, n_dev - 1)], send_sem=s_sem, recv_sem=r_sem,
        device_id=target(1), device_id_type=MESH)
    rest.wait_recv()
    everyone = seen[...].reshape(n_dev * 8, lanes).astype(BF16)
    loads = dot(everyone, one_hot(same_plane))
    peak_ref[...] = jnp.broadcast_to(jnp.max(loads, axis=0, keepdims=True), peak_ref.shape)
    sources = jnp.concatenate([seen[peer_of(me_z, k) * NC + me_c] for k in range(NZ)], axis=0).astype(BF16)
    lane_of, slot_of = iota((lanes, SLOTS), 0), iota((lanes, SLOTS), 1)
    within = iota((NZ * 8, SLOTS), 1) % CAP
    for layer in range(n_layers):
        for mb in range(n_mb):
            first = (layer * n_mb + mb) * EXPERTS + me_z * NC
            own = lane_of - first
            amount = dot(sources, one_hot(own == slot_of // CAP)).astype(jnp.int32)
            ahead = dot(sources, one_hot((own >= 0) & (own < slot_of // CAP))).astype(jnp.int32)
            prow_ref[layer, mb] = jnp.where(within < amount, ahead + within, -1).reshape(NZ, 8, SLOTS)
    rest.wait_send()


def moe_kernel(rows, tok_ref, meta_ref, prow_ref, gate_ref, w1_hbm, w3_hbm, wd_hbm, out_ref,
               ucur, pmeta, tsend, trecv, tfull, ssend, xrecv, osend, rrecv, ysend, yrecv, w1, w3, wd, hid,
               w_sem, m_sem, tz_s, tz_r, tf_s, tf_r, sp_s, sp_r, op_s, op_r, yz_s, yz_r):
    n_layers, n_mb = meta_ref.shape[0], meta_ref.shape[1]
    n_tok, width = ucur.shape[1:]
    ffn = w1.shape[-1]
    me_z, me_c = place()
    peer_z = functools.partial(peer_of, me_z)

    def peer_c(d):
        return (me_c + d) % NC

    def w_copies(layer):
        return [pltpu.make_async_copy(src.at[layer, 0], dst, w_sem.at[i])
                for i, (src, dst) in enumerate(((w1_hbm, w1), (w3_hbm, w3), (wd_hbm, wd)))]

    meta_copy = pltpu.make_async_remote_copy(
        src_ref=meta_ref, dst_ref=pmeta, send_sem=m_sem.at[0], recv_sem=m_sem.at[1],
        device_id={"ez": peer_z(2)}, device_id_type=MESH)

    def t_copy(mb, i):
        return pltpu.make_async_remote_copy(
            src_ref=tsend.at[mb, i], dst_ref=trecv.at[mb, i], send_sem=tz_s.at[mb, i], recv_sem=tz_r.at[mb, i],
            device_id={"ez": peer_z(1)}, device_id_type=MESH)

    def full_copy(mb):
        return pltpu.make_async_remote_copy(
            src_ref=ucur.at[mb], dst_ref=tfull.at[mb], send_sem=tf_s.at[mb], recv_sem=tf_r.at[mb],
            device_id={"ez": peer_z(2)}, device_id_type=MESH)

    def y_copy(mb, k):
        return pltpu.make_async_remote_copy(
            src_ref=ysend.at[mb, k], dst_ref=yrecv.at[mb, me_z], send_sem=yz_s.at[mb, k], recv_sem=yz_r.at[mb, me_z],
            device_id={"ez": peer_z(k)}, device_id_type=MESH)

    def y_wait(mb, k):
        src = peer_z(k)
        pltpu.make_async_remote_copy(
            src_ref=ysend.at[mb, k], dst_ref=yrecv.at[mb, src], send_sem=yz_s.at[mb, k], recv_sem=yz_r.at[mb, src],
            device_id={"ez": src}, device_id_type=MESH).wait_recv()

    def plane_copy(src, dst, s_sem, r_sem, mb, k, d):
        c = peer_c(d)
        return pltpu.make_async_remote_copy(
            src_ref=src.at[mb, k, c], dst_ref=dst.at[mb, k, me_c], send_sem=s_sem.at[mb, k], recv_sem=r_sem.at[mb, k],
            device_id=plane_id(c), device_id_type=MESH)

    def plane_all(src, dst, s_sem, r_sem, mb, k):
        part = pl.ds(0, NC - 1)
        return pltpu.make_async_remote_copy(
            src_ref=src.at[mb, k, part], dst_ref=dst.at[mb, k, part], send_sem=s_sem.at[mb, k],
            recv_sem=r_sem.at[mb, k], device_id=plane_id(peer_c(1)), device_id_type=MESH)

    def choose(ref, layer, mb, j, n, base):
        row = iota((n, n_tok), 0) + base
        return one_hot((row == ref[layer, mb, j:j + 1, :]) | (row == ref[layer, mb, j + 1:j + 2, :]))

    def send_tokens(layer, mb):
        full_copy(mb).start()
        tsend[mb, 0] = dot(choose(meta_ref, layer, mb, 0, rows, peer_z(1) * SLOTS), ucur[mb]).astype(BF16)
        t_copy(mb, 0).start()

    def packing(layer, mb, k):
        return one_hot(iota((rows, SLOTS), 0) == prow_ref[layer, mb, k, 0:1, :])

    def expand(layer, mb, k):
        if k == 0:
            block = dot(choose(meta_ref, layer, mb, 2, SLOTS, me_z * SLOTS), ucur[mb])
        elif k == 2:
            full_copy(mb).wait_recv()
            tsend[mb, 1] = dot(choose(pmeta, layer, mb, 0, rows, peer_z(1) * SLOTS), tfull[mb]).astype(BF16)
            t_copy(mb, 1).start()
            block = dot(choose(pmeta, layer, mb, 2, SLOTS, me_z * SLOTS), tfull[mb])
        else:
            t_copy(mb, k // 2).wait_recv()
            block = dot_t(packing(layer, mb, k), trecv[mb, k // 2])
        ssend[mb, k] = block.astype(BF16).reshape(NC, CAP, width)
        for d in range(1, NC):
            plane_copy(ssend, xrecv, sp_s, sp_r, mb, k, d).start()
        xrecv[mb, k, me_c] = ssend[mb, k, me_c]

    def expert(mb, k):
        plane_all(ssend, xrecv, sp_s, sp_r, mb, k).wait_recv()

        def up(t, _):
            cols = pl.ds(pl.multiple_of(t * TILE, TILE), TILE)
            x = xrecv[mb, k].reshape(SLOTS, width)
            a = dot(x, w1[:, cols])
            b = dot(x, w3[:, cols])
            hid[:, cols] = (jax.nn.silu(a) * b).astype(BF16)
            return 0

        lax.fori_loop(0, ffn // TILE, up, 0, unroll=True)

        def down(t, _):
            cols = pl.ds(pl.multiple_of(t * TILE, TILE), TILE)
            osend[mb, k, :, :, cols] = dot(hid[...], wd[:, cols]).astype(BF16).reshape(NC, CAP, TILE)
            return 0

        lax.fori_loop(0, width // TILE, down, 0, unroll=True)
        for d in range(1, NC):
            plane_copy(osend, rrecv, op_s, op_r, mb, k, d).start()
        rrecv[mb, k, me_c] = osend[mb, k, me_c]

    def give_back(layer, mb, k):
        plane_all(osend, rrecv, op_s, op_r, mb, k).wait_recv()
        packed = dot(packing(layer, mb, k), rrecv[mb, k].reshape(SLOTS, width)).astype(BF16)

        @pl.when(k == 0)
        def _():
            yrecv[mb, me_z] = packed

        @pl.when(k > 0)
        def _():
            ysend[mb, k] = packed
            y_copy(mb, k).start()

    def combine(layer, mb):
        full_copy(mb).wait_send()
        for k in (1, 2, 3):
            y_wait(mb, k)
        y = yrecv[mb].reshape(NZ * rows, width)
        shape = (NZ, rows, n_tok)
        row = (iota(shape, 0) * SLOTS + iota(shape, 1)).reshape(NZ * rows, n_tok)
        total = jnp.zeros((n_tok, width), F32)
        for j in range(2):
            picked = dot_t(one_hot(row == meta_ref[layer, mb, j:j + 1, :]), y)
            total = total + gate_ref[layer, mb, :, j:j + 1] * picked
        ucur[mb] = (ucur[mb].astype(F32) + ROUTE_SCALE * total).astype(BF16)
        for i in range(2):
            t_copy(mb, i).wait_send()
        for k in range(NZ):
            if k:
                y_copy(mb, k).wait_send()
            plane_all(ssend, xrecv, sp_s, sp_r, mb, k).wait_send()
            plane_all(osend, rrecv, op_s, op_r, mb, k).wait_send()

    barrier = pltpu.get_barrier_semaphore()
    for k in range(1, NZ):
        pl.semaphore_signal(barrier, inc=1, device_id={"ez": peer_z(k)}, device_id_type=MESH)
    for d in range(1, NC):
        pl.semaphore_signal(barrier, inc=1, device_id=plane_id(peer_c(d)), device_id_type=MESH)
    for copy in w_copies(0):
        copy.start()
    ucur[...] = tok_ref[...]
    pl.semaphore_wait(barrier, NZ - 1 + NC - 1)
    meta_copy.start()
    for mb in range(n_mb):
        send_tokens(0, mb)
    meta_copy.wait_recv()
    n_step = n_mb * NZ

    def layer_step(layer, _):
        expand(layer, 0, 0)

        def step(j, _):
            for k in range(NZ):
                @pl.when((j + 1 < n_step) & ((j + 1) % NZ == k))
                def _():
                    expand(layer, (j + 1) // NZ, k)

            @pl.when(j == 0)
            def _():
                for copy in w_copies(layer):
                    copy.wait()

            expert(j // NZ, j % NZ)

            @pl.when((j == n_step - 1) & (layer + 1 < n_layers))
            def _():
                for copy in w_copies(layer + 1):
                    copy.start()

            @pl.when(j > 0)
            def _():
                give_back(layer, (j - 1) // NZ, (j - 1) % NZ)
            return 0

        lax.fori_loop(0, n_step, step, 0)
        give_back(layer, n_mb - 1, NZ - 1)

        for mb in range(n_mb):
            combine(layer, mb)

            @pl.when(layer + 1 < n_layers)
            def _():
                send_tokens(layer + 1, mb)
        return 0

    lax.fori_loop(0, n_layers, layer_step, 0)
    meta_copy.wait_send()
    out_ref[...] = ucur[...]


VMEM_SPEC = pl.BlockSpec(memory_space=pltpu.VMEM)


def run_route(ids):
    n_layers, n_mb, n_tok, top_k = ids.shape
    lanes = n_layers * n_mb * EXPERTS
    return pl.pallas_call(
        route_kernel,
        out_shape=(jax.ShapeDtypeStruct((n_layers, n_mb, 2 * top_k, n_tok), jnp.int32),
                   jax.ShapeDtypeStruct((n_layers, n_mb, NZ, 8, SLOTS), jnp.int32),
                   jax.ShapeDtypeStruct((8, lanes), F32)),
        in_specs=[VMEM_SPEC],
        out_specs=(VMEM_SPEC,) * 3,
        scratch_shapes=[pltpu.VMEM((8, lanes), F32), pltpu.VMEM((NZ * NC, 8, lanes), F32),
                        pltpu.SemaphoreType.DMA, pltpu.SemaphoreType.DMA],
        compiler_params=pltpu.CompilerParams(collective_id=0, has_side_effects=True),
        name="route",
    )(ids)


def run_moe(rows, collective_id, tokens, meta, prow, gates, w_up1, w_up3, w_down):
    n_mb, n_tok, width = tokens.shape
    ffn = w_up1.shape[-1]
    hbm = pl.BlockSpec(memory_space=pl.ANY)
    per_mb = pltpu.VMEM((n_mb, n_tok, width), BF16)
    relay = pltpu.VMEM((n_mb, 2, rows, width), BF16)
    packed = pltpu.VMEM((n_mb, NZ, rows, width), BF16)
    padded = pltpu.VMEM((n_mb, NZ, NC, CAP, width), BF16)
    pair = pltpu.SemaphoreType.DMA((n_mb, NZ))
    return pl.pallas_call(
        functools.partial(moe_kernel, rows),
        out_shape=jax.ShapeDtypeStruct(tokens.shape, BF16),
        in_specs=[VMEM_SPEC] * 4 + [hbm] * 3,
        out_specs=VMEM_SPEC,
        scratch_shapes=[
            per_mb, pltpu.VMEM(meta.shape, jnp.int32), relay, relay, per_mb,
            padded, padded, padded, padded, packed, packed,
            pltpu.VMEM((width, ffn), BF16), pltpu.VMEM((width, ffn), BF16), pltpu.VMEM((ffn, width), BF16),
            pltpu.VMEM((SLOTS, ffn), BF16),
            pltpu.SemaphoreType.DMA((3,)), pltpu.SemaphoreType.DMA((2,)),
            pltpu.SemaphoreType.DMA((n_mb, 2)), pltpu.SemaphoreType.DMA((n_mb, 2)),
            pltpu.SemaphoreType.DMA((n_mb,)), pltpu.SemaphoreType.DMA((n_mb,)),
        ] + [pair] * 6,
        compiler_params=pltpu.CompilerParams(
            collective_id=collective_id, has_side_effects=True, vmem_limit_bytes=67_000_000),
        name=f"moe_rows_{rows}",
    )(tokens, meta, prow, gates, w_up1, w_up3, w_down)


def solution(mesh):
    tok_spec = P(None, MESH_AXES, None)
    route_spec = P(None, None, MESH_AXES, None)
    weight_spec = P(None, MESH_AXES, None, None)

    def device_body(tokens_in, expert_ids, gate_vals, w_up1, w_up3, w_down):
        meta, prow, peak = run_route(expert_ids)

        def branch(rows, collective_id):
            return lambda: run_moe(rows, collective_id, tokens_in, meta, prow, gate_vals, w_up1, w_up3, w_down)

        return lax.cond(jnp.max(peak) <= 176.0, branch(176, 1), branch(SLOTS, 2))

    return jax.shard_map(device_body, mesh=mesh, in_specs=(tok_spec, route_spec, route_spec, weight_spec, weight_spec, weight_spec), out_specs=tok_spec, check_vma=False)
```

time: 385 us -> 315 us (0.82)
  blocking collectives: 44 us -> 0 us
  Pallas kernels: 319 us -> 301 us
  other arithmetic: 10.1 us -> 1.28 us
    all_gather x1 -> x0, blocking collectives: 44 us -> none  [device_body(): all_counts = lax.all_gather(by_plane, MESH_AXES)]
    pallas_call x1, Pallas kernels: 319 us -> 289 us  [run_moe(): pl.pallas_call(functools.partial(moe_kernel, rows), out_shape=jax.ShapeDt...]
    pallas_call x0 -> x1, Pallas kernels: none -> 12 us  [run_route(): pl.pallas_call(route_kernel, out_shape=(jax.ShapeDtypeStruct((n_layers, n...]
    reduce_sum x3 -> x0, other arithmetic: 3.89 us -> none  [the longest x1 2.33 us: device_body(): fits = jnp.max(jnp.sum(all_counts, axis=-1)) <= 176]
where the time goes in v2:
time: 315 us; the launch traced here: 309 us
  Pallas kernels  301 us (96%)
  local copies, waits for them, and re-layouts  5.7 us (2%)
    pallas_call x1, Pallas kernels, run_moe(): pl.pallas_call(functools.partial(moe_kernel, rows), out_shape=jax.ShapeDt...  289 us
    pallas_call x1, Pallas kernels, run_route(): pl.pallas_call(route_kernel, out_shape=(jax.ShapeDtypeStruct((n_layers, n...  12 us

profile of v2, /device:TPU:0, one launch (start us, length us, event | category | flops | bytes accessed | tf_op | source)
XLA Modules:
  0.0 308.9 jit_solution(15973872530698255405)
XLA Ops:
  0.0 1.7 copy.9.ids_ref
  1.7 12.0 %route.1 = (s32[2,2,4,256]{3,2,1,0:T(4,128)S(1)}, s32[2,2,4,8,256]{4,3,2,1,0:T(8,128)}, f32[8,128]{1,0:T(8,128)}) custom-call(s32[2,2,256,2]{3,2,1,0:T(8,128)} %copy.9.ids_ref), custom_call_target="tpu_custom_call" | custom-call | tf_op jit(solution)/shard_map/route/pallas_call | solution.py:327
  13.8 1.3 reduce_max.9
  15.7 291.0 %conditional.1 = (bf16[2,256,1024]{2,1,0:T(8,128)(2,1)}) conditional(s32[]{:T(128)} %convert_element_type.3, (bf16[2,256,1024]{2,1,0:T(8,128)(2,1)}, s32[2,2,4,256]{3,2,1,0:T(4,128)S(1)}, s32[2,2,4,8,256]{4,3,2,1,0:T(8,128)}, f32[2,2,256,2]{2,3,1,0:T(2,128)}, bf16[2,1,1024,2816]{3,2,1,0:T(8,128)(2,1)}, ...), branch_computations={%region_1.0_spmd, %region_2.0_spmd} | conditional | bytes 16392 | solution.py:381
  15.9 1.7 copy.11.gate_ref
  17.6 289.0 %moe_rows_176.1 = bf16[2,256,1024]{2,1,0:T(8,128)(2,1)} custom-call(bf16[2,256,1024]{2,1,0:T(8,128)(2,1)} %get-tuple-element.43.tok_ref, s32[2,2,4,256]{3,2,1,0:T(4,128)S(1)} %get-tuple-element.44.meta_ref, s32[2,2,4,8,256]{4,3,2,1,0:T(8,128)} %get-tuple-element.45.prow_ref, f32[2,2,256,2]{3,2,1,0:T(8,128)} %copy.11.gate_ref, ...), custom_call_target="tpu_custom_call" | custom-call | tf_op jit(solution)/shard_map/cond/branch_1_fun/moe_rows_176/pallas_call | solution.py:350
  306.7 2.3 copy.15

commit v3 on v2

v3 whole, which is shorter than its diff:
```python
import functools

import jax
import jax.numpy as jnp
from jax import lax
from jax.experimental import pallas as pl
from jax.experimental.pallas import tpu as pltpu
from jax.sharding import PartitionSpec as P

ROUTE_SCALE = 2.5
MESH_AXES = ("ez", "ey", "ex")
NZ, NC, CAP = 4, 8, 32
EXPERTS, SLOTS = NZ * NC, NC * CAP
TILE = 256
BF16, F32 = jnp.bfloat16, jnp.float32
MESH = pl.DeviceIdType.MESH


def dot(lhs, rhs):
    return jnp.dot(lhs, rhs, preferred_element_type=F32)


def dot_t(lhs, rhs):
    return lax.dot_general(lhs, rhs, (((0,), (0,)), ((), ())), preferred_element_type=F32)


def dot_nt(lhs, rhs):
    return lax.dot_general(lhs, rhs, (((1,), (1,)), ((), ())), preferred_element_type=F32)


def one_hot(cond):
    return jnp.where(cond, 1.0, 0.0).astype(BF16)


def iota(shape, dim):
    return lax.broadcasted_iota(jnp.int32, shape, dim)


def place():
    return lax.axis_index("ez"), lax.axis_index("ey") * 4 + lax.axis_index("ex")


def source_of(me_z, k):
    half, far = me_z // 2, k // 2
    near = (1 - k) * me_z + k * (4 * half + 1 - me_z)
    away = (3 - k) * (2 - half) + (k - 2) * (3 - 3 * half)
    return (1 - far) * near + far * away


def plane_id(c):
    return {"ey": c // 4, "ex": c % 4}


def route_kernel(ids_ref, meta_ref, prow_ref, peak_ref, mine, seen, s_sem, r_sem):
    n_layers, n_mb, top_k, n_tok = ids_ref.shape
    n_set = n_layers * n_mb
    lanes = n_set * EXPERTS
    me_z, me_c = place()
    me = me_z * NC + me_c
    n_dev = NZ * NC

    def target(d):
        dev = (me + d) % n_dev
        return {"ez": dev // NC, "ey": dev % NC // 4, "ex": dev % 4}

    barrier = pltpu.get_barrier_semaphore()

    def greet(d, _):
        pl.semaphore_signal(barrier, inc=1, device_id=target(d), device_id_type=MESH)
        return 0

    lax.fori_loop(1, n_dev, greet, 0)

    expert = iota((EXPERTS, n_tok), 0)
    chosen = [jnp.concatenate([jnp.where(ids_ref[i // n_mb, i % n_mb, j:j + 1, :] == expert, 1.0, 0.0)
                               for i in range(n_set)], axis=0) for j in range(top_k)]
    per_tok = (chosen[0] + chosen[1]).astype(BF16)
    counts = dot_nt(jnp.ones((8, n_tok), BF16), per_tok)
    mine[...] = counts
    seen[me] = counts
    pl.semaphore_wait(barrier, n_dev - 1)

    def share(d, _):
        pltpu.make_async_remote_copy(src_ref=mine, dst_ref=seen.at[me], send_sem=s_sem, recv_sem=r_sem,
                                     device_id=target(d), device_id_type=MESH).start()
        return 0

    lax.fori_loop(1, n_dev, share, 0)

    rank = dot(per_tok, one_hot(iota((n_tok, n_tok), 0) < iota((n_tok, n_tok), 1)))
    totals = dot(per_tok, jnp.ones((n_tok, n_tok), BF16)).astype(BF16)
    row, col = iota((lanes, lanes), 0), iota((lanes, lanes), 1)
    same_plane = row // NC == col // NC
    start = dot(one_hot(same_plane & (col < row)), totals)
    which = iota((lanes, n_tok), 0) % EXPERTS
    base = which // NC * SLOTS
    packed = base.astype(F32) + rank + start
    padded = (base + which % NC * CAP).astype(F32) + rank
    for j in range(top_k):
        for i in range(n_set):
            part = slice(i * EXPERTS, (i + 1) * EXPERTS)
            for place_of, at in ((packed, j), (padded, top_k + j)):
                found = jnp.sum(chosen[j][part] * place_of[part], axis=0, keepdims=True)
                meta_ref[i // n_mb, i % n_mb, at:at + 1, :] = found.astype(jnp.int32)

    rest = pltpu.make_async_remote_copy(
        src_ref=seen.at[pl.ds(0, n_dev - 1)], dst_ref=seen.at[pl.ds(0, n_dev - 1)], send_sem=s_sem, recv_sem=r_sem,
        device_id=target(1), device_id_type=MESH)
    rest.wait_recv()
    everyone = seen[...].reshape(n_dev * 8, lanes).astype(BF16)
    loads = dot(everyone, one_hot(same_plane))
    peak_ref[0] = jnp.max(loads)
    sources = jnp.concatenate([seen[source_of(me_z, k) * NC + me_c] for k in range(NZ)], axis=0).astype(BF16)
    lane_of, slot_of = iota((lanes, SLOTS), 0), iota((lanes, SLOTS), 1)
    within = iota((NZ * 8, SLOTS), 1) % CAP
    for i in range(n_set):
        own = lane_of - (i * EXPERTS + me_z * NC)
        amount = dot(sources, one_hot(own == slot_of // CAP)).astype(jnp.int32)
        ahead = dot(sources, one_hot((own >= 0) & (own < slot_of // CAP))).astype(jnp.int32)
        prow_ref[i // n_mb, i % n_mb] = jnp.where(within < amount, ahead + within, -1).reshape(NZ, 8, SLOTS)
    rest.wait_send()


def moe_kernel(rows, tok_ref, meta_ref, prow_ref, gate_ref, w1_hbm, w3_hbm, wd_hbm, out_ref,
               ucur, gcol, pmeta, tsend, trecv, tfull, ssend, xrecv, osend, rrecv, ysend, yrecv, w1, w3, wd, hid,
               w_sem, m_s, m_r, tz_s, tz_r, tf_s, tf_r, sp_s, sp_r, op_s, op_r, yz_s, yz_r):
    n_layers, n_mb = meta_ref.shape[0], meta_ref.shape[1]
    n_tok, width = ucur.shape[1:]
    ffn = w1.shape[-1]
    me_z, me_c = place()
    source = functools.partial(source_of, me_z)
    near = source(1)
    gateway = source(2)
    inner = (me_z + 1) // 2 % 2
    my_far = 1 - inner

    def peer_c(d):
        return (me_c + d) % NC

    def w_copies(layer):
        return [pltpu.make_async_copy(src.at[layer, 0], dst, w_sem.at[i])
                for i, (src, dst) in enumerate(((w1_hbm, w1), (w3_hbm, w3), (wd_hbm, wd)))]

    def meta_copy(i):
        return pltpu.make_async_remote_copy(
            src_ref=meta_ref, dst_ref=pmeta.at[i], send_sem=m_s.at[0], recv_sem=m_r.at[i],
            device_id={"ez": gateway}, device_id_type=MESH)

    def t_copy(mb, i):
        return pltpu.make_async_remote_copy(
            src_ref=tsend.at[mb, i], dst_ref=trecv.at[mb, i], send_sem=tz_s.at[mb, i], recv_sem=tz_r.at[mb, i],
            device_id={"ez": near}, device_id_type=MESH)

    def full_copy(mb, i):
        return pltpu.make_async_remote_copy(
            src_ref=ucur.at[mb], dst_ref=tfull.at[mb, i], send_sem=tf_s.at[mb], recv_sem=tf_r.at[mb, i],
            device_id={"ez": gateway}, device_id_type=MESH)

    def y_copy(mb, k):
        return pltpu.make_async_remote_copy(
            src_ref=ysend.at[mb, k], dst_ref=yrecv.at[mb, me_z], send_sem=yz_s.at[mb, k], recv_sem=yz_r.at[mb, me_z],
            device_id={"ez": source(k)}, device_id_type=MESH)

    def y_wait(mb, k):
        src = source(k)
        pltpu.make_async_remote_copy(
            src_ref=ysend.at[mb, k], dst_ref=yrecv.at[mb, src], send_sem=yz_s.at[mb, k], recv_sem=yz_r.at[mb, src],
            device_id={"ez": src}, device_id_type=MESH).wait_recv()

    def plane_copy(src, dst, s_sem, r_sem, mb, k, d):
        c = peer_c(d)
        return pltpu.make_async_remote_copy(
            src_ref=src.at[mb, k, c], dst_ref=dst.at[mb, k, me_c], send_sem=s_sem.at[mb, k], recv_sem=r_sem.at[mb, k],
            device_id=plane_id(c), device_id_type=MESH)

    def plane_all(src, dst, s_sem, r_sem, mb, k):
        part = pl.ds(0, NC - 1)
        return pltpu.make_async_remote_copy(
            src_ref=src.at[mb, k, part], dst_ref=dst.at[mb, k, part], send_sem=s_sem.at[mb, k],
            recv_sem=r_sem.at[mb, k], device_id=plane_id(peer_c(1)), device_id_type=MESH)

    def choose(ref, j, n, base):
        row = iota((n, n_tok), 0) + base
        return one_hot((row == ref[j:j + 1, :]) | (row == ref[j + 1:j + 2, :]))

    def send_tokens(layer, mb):
        tsend[mb, 0] = dot(choose(meta_ref.at[layer, mb], 0, rows, near * SLOTS), ucur[mb]).astype(BF16)
        t_copy(mb, 0).start()
        full_copy(mb, my_far).start()

    def packing(layer, mb, k):
        return one_hot(iota((rows, SLOTS), 0) == prow_ref[layer, mb, k, 0:1, :])

    def spread(mb, k, block):
        ssend[mb, k] = block.astype(BF16).reshape(NC, CAP, width)
        for d in range(1, NC):
            plane_copy(ssend, xrecv, sp_s, sp_r, mb, k, d).start()
        xrecv[mb, k, me_c] = ssend[mb, k, me_c]

    def expand_own(layer, mb):
        spread(mb, 0, dot(choose(meta_ref.at[layer, mb], 2, SLOTS, me_z * SLOTS), ucur[mb]))

    def expand(layer, mb, k):
        def from_packed():
            t_copy(mb, k - 1).wait_recv()
            spread(mb, k, dot_t(packing(layer, mb, k), trecv[mb, k - 1]))

        @pl.when((k == 1) | (inner == 0))
        def _():
            from_packed()

        @pl.when((k > 1) & (inner == 1))
        def _():
            i = k - 2
            full_copy(mb, i).wait_recv()
            tsend[mb, k - 1] = dot(choose(pmeta.at[i, layer, mb], 0, rows, near * SLOTS), tfull[mb, i]).astype(BF16)
            t_copy(mb, k - 1).start()
            spread(mb, k, dot(choose(pmeta.at[i, layer, mb], 2, SLOTS, me_z * SLOTS), tfull[mb, i]))

    def expert(mb, k):
        plane_all(ssend, xrecv, sp_s, sp_r, mb, k).wait_recv()

        def up(t, _):
            cols = pl.ds(pl.multiple_of(t * TILE, TILE), TILE)
            x = xrecv[mb, k].reshape(SLOTS, width)
            a = dot(x, w1[:, cols])
            b = dot(x, w3[:, cols])
            hid[:, cols] = (jax.nn.silu(a) * b).astype(BF16)
            return 0

        lax.fori_loop(0, ffn // TILE, up, 0, unroll=True)

        def down(t, _):
            cols = pl.ds(pl.multiple_of(t * TILE, TILE), TILE)
            osend[mb, k, :, :, cols] = dot(hid[...], wd[:, cols]).astype(BF16).reshape(NC, CAP, TILE)
            return 0

        lax.fori_loop(0, width // TILE, down, 0, unroll=True)
        for d in range(1, NC):
            plane_copy(osend, rrecv, op_s, op_r, mb, k, d).start()
        rrecv[mb, k, me_c] = osend[mb, k, me_c]

    def give_back(layer, mb, k):
        plane_all(osend, rrecv, op_s, op_r, mb, k).wait_recv()
        packed = dot(packing(layer, mb, k), rrecv[mb, k].reshape(SLOTS, width)).astype(BF16)

        @pl.when(k == 0)
        def _():
            yrecv[mb, me_z] = packed

        @pl.when(k > 0)
        def _():
            ysend[mb, k] = packed
            y_copy(mb, k).start()

    def combine(layer, mb):
        full_copy(mb, my_far).wait_send()
        for k in (1, 2, 3):
            y_wait(mb, k)
        y = yrecv[mb].reshape(NZ * rows, width)
        shape = (NZ, rows, n_tok)
        row = (iota(shape, 0) * SLOTS + iota(shape, 1)).reshape(NZ * rows, n_tok)
        total = jnp.zeros((n_tok, width), F32)
        for j in range(2):
            picked = dot_t(one_hot(row == meta_ref[layer, mb, j:j + 1, :]), y)
            total = total + gcol[layer, :, 2 * mb + j:2 * mb + j + 1] * picked
        ucur[mb] = (ucur[mb].astype(F32) + ROUTE_SCALE * total).astype(BF16)
        t_copy(mb, 0).wait_send()

        @pl.when(inner == 1)
        def _():
            for i in (1, 2):
                t_copy(mb, i).wait_send()

        for k in range(NZ):
            if k:
                y_copy(mb, k).wait_send()
            plane_all(ssend, xrecv, sp_s, sp_r, mb, k).wait_send()
            plane_all(osend, rrecv, op_s, op_r, mb, k).wait_send()

    barrier = pltpu.get_barrier_semaphore()
    for k in range(1, NZ):
        pl.semaphore_signal(barrier, inc=1, device_id={"ez": source(k)}, device_id_type=MESH)
    for d in range(1, NC):
        pl.semaphore_signal(barrier, inc=1, device_id=plane_id(peer_c(d)), device_id_type=MESH)
    for copy in w_copies(0):
        copy.start()
    ucur[...] = tok_ref[...]
    n_gate = 2 * n_mb
    turned = jnp.transpose(gate_ref[...].reshape(n_layers * n_gate, n_tok))
    for layer in range(n_layers):
        gcol[layer] = turned[:, layer * n_gate:(layer + 1) * n_gate]
    pl.semaphore_wait(barrier, NZ - 1 + NC - 1)
    meta_copy(my_far).start()
    for mb in range(n_mb):
        send_tokens(0, mb)

    @pl.when(inner == 1)
    def _():
        for i in range(2):
            meta_copy(i).wait_recv()

    n_step = n_mb * NZ

    def chunk(j):
        later = (j + 6) // 8
        return later * ((j + 1) // 3 - 1) + (1 - later) * j, later * (1 + (j + 1) % 3)

    def layer_step(layer, _):
        for mb in range(n_mb):
            expand_own(layer, mb)
        for copy in w_copies(layer):
            copy.wait()

        def step(j, _):
            expert(*chunk(j))

            @pl.when((j == n_step - 1) & (layer + 1 < n_layers))
            def _():
                for copy in w_copies(layer + 1):
                    copy.start()

            @pl.when(j > 0)
            def _():
                give_back(layer, *chunk(j - 1))

            @pl.when(j + 2 < n_step)
            def _():
                expand(layer, *chunk(j + 2))
            return 0

        lax.fori_loop(0, n_step, step, 0)
        give_back(layer, n_mb - 1, NZ - 1)

        for mb in range(n_mb):
            combine(layer, mb)

            @pl.when(layer + 1 < n_layers)
            def _():
                send_tokens(layer + 1, mb)
        return 0

    lax.fori_loop(0, n_layers, layer_step, 0)
    meta_copy(my_far).wait_send()
    out_ref[...] = ucur[...]


VMEM_SPEC = pl.BlockSpec(memory_space=pltpu.VMEM)


def run_route(ids):
    n_layers, n_mb, top_k, n_tok = ids.shape
    lanes = n_layers * n_mb * EXPERTS
    return pl.pallas_call(
        route_kernel,
        out_shape=(jax.ShapeDtypeStruct((n_layers, n_mb, 2 * top_k, n_tok), jnp.int32),
                   jax.ShapeDtypeStruct((n_layers, n_mb, NZ, 8, SLOTS), jnp.int32),
                   jax.ShapeDtypeStruct((1,), F32)),
        in_specs=[VMEM_SPEC],
        out_specs=(VMEM_SPEC, VMEM_SPEC, pl.BlockSpec(memory_space=pltpu.SMEM)),
        scratch_shapes=[pltpu.VMEM((8, lanes), F32), pltpu.VMEM((NZ * NC, 8, lanes), F32),
                        pltpu.SemaphoreType.DMA, pltpu.SemaphoreType.DMA],
        compiler_params=pltpu.CompilerParams(collective_id=0, has_side_effects=True),
        name="route",
    )(ids)


def run_moe(rows, collective_id, tokens, meta, prow, gates, w_up1, w_up3, w_down):
    n_mb, n_tok, width = tokens.shape
    ffn = w_up1.shape[-1]
    hbm = pl.BlockSpec(memory_space=pl.ANY)
    per_mb = pltpu.VMEM((n_mb, n_tok, width), BF16)
    relay = pltpu.VMEM((n_mb, 3, rows, width), BF16)
    packed = pltpu.VMEM((n_mb, NZ, rows, width), BF16)
    padded = pltpu.VMEM((n_mb, NZ, NC, CAP, width), BF16)
    pair = pltpu.SemaphoreType.DMA((n_mb, NZ))
    return pl.pallas_call(
        functools.partial(moe_kernel, rows),
        out_shape=jax.ShapeDtypeStruct(tokens.shape, BF16),
        in_specs=[VMEM_SPEC] * 4 + [hbm] * 3,
        out_specs=VMEM_SPEC,
        scratch_shapes=[
            per_mb, pltpu.VMEM((meta.shape[0], n_tok, 2 * n_mb), F32), pltpu.VMEM((2,) + meta.shape, jnp.int32),
            relay, relay, pltpu.VMEM((n_mb, 2, n_tok, width), BF16),
            padded, padded, padded, padded, packed, packed,
            pltpu.VMEM((width, ffn), BF16), pltpu.VMEM((width, ffn), BF16), pltpu.VMEM((ffn, width), BF16),
            pltpu.VMEM((SLOTS, ffn), BF16),
            pltpu.SemaphoreType.DMA((3,)), pltpu.SemaphoreType.DMA((1,)), pltpu.SemaphoreType.DMA((2,)),
            pltpu.SemaphoreType.DMA((n_mb, 3)), pltpu.SemaphoreType.DMA((n_mb, 3)),
            pltpu.SemaphoreType.DMA((n_mb,)), pltpu.SemaphoreType.DMA((n_mb, 2)),
        ] + [pair] * 6,
        compiler_params=pltpu.CompilerParams(
            collective_id=collective_id, has_side_effects=True, vmem_limit_bytes=67_000_000),
        name=f"moe_rows_{rows}",
    )(tokens, meta, prow, gates, w_up1, w_up3, w_down)


def solution(mesh):
    tok_spec = P(None, MESH_AXES, None)
    route_spec = P(None, None, MESH_AXES, None)
    weight_spec = P(None, MESH_AXES, None, None)

    def device_body(tokens_in, expert_ids, gate_vals, w_up1, w_up3, w_down):
        meta, prow, peak = run_route(expert_ids.transpose(0, 1, 3, 2))
        gates = gate_vals.transpose(0, 1, 3, 2)

        def branch(rows, collective_id):
            return lambda: run_moe(rows, collective_id, tokens_in, meta, prow, gates, w_up1, w_up3, w_down)

        return lax.cond(peak[0] <= 176.0, branch(176, 1), branch(SLOTS, 2))

    return jax.shard_map(device_body, mesh=mesh, in_specs=(tok_spec, route_spec, route_spec, weight_spec, weight_spec, weight_spec), out_specs=tok_spec, check_vma=False)
```

time: 315 us -> 265 us (0.84); the launches traced: 309 us -> 265 us
  Pallas kernels: 301 us -> 262 us
  local copies, waits for them, and re-layouts: 5.7 us -> 2.26 us
    pallas_call x1, Pallas kernels: 289 us -> 250 us  [run_moe(): pl.pallas_call(functools.partial(moe_kernel, rows), out_shape=jax.ShapeDt...]
where the time goes in v3:
time: 265 us
  Pallas kernels  262 us (99%)
    pallas_call x1, Pallas kernels, run_moe(): pl.pallas_call(functools.partial(moe_kernel, rows), out_shape=jax.ShapeDt...  250 us
    pallas_call x1, Pallas kernels, run_route(): pl.pallas_call(route_kernel, out_shape=(jax.ShapeDtypeStruct((n_layers, n...  11.7 us

profile of v3, /device:TPU:0, one launch (start us, length us, event | category | flops | bytes accessed | tf_op | source)
XLA Modules:
  0.0 264.9 jit_solution(6879002197021447086)
XLA Ops:
  0.0 11.7 %route.1 = (s32[2,2,4,256]{3,2,1,0:T(4,128)S(1)}, s32[2,2,4,8,256]{4,3,2,1,0:T(8,128)}, f32[1]{0:T(128)}) custom-call(s32[2,2,2,256]{3,2,1,0:T(2,128)} %bitcast.5), custom_call_target="tpu_custom_call" | custom-call | tf_op jit(solution)/shard_map/route/pallas_call | solution.py:354
  12.3 250.3 %conditional.1 = (bf16[2,256,1024]{2,1,0:T(8,128)(2,1)}) conditional(s32[]{:T(128)} %bitcast.1, (bf16[2,256,1024]{2,1,0:T(8,128)(2,1)}, s32[2,2,4,256]{3,2,1,0:T(4,128)S(1)}, s32[2,2,4,8,256]{4,3,2,1,0:T(8,128)}, f32[2,2,2,256]{3,2,1,0:T(2,128)}, bf16[2,1,1024,2816]{3,2,1,0:T(8,128)(2,1)}, /*index=5*/bf16[2,1,1024,2816]{3,2,1,0:T(8,128)(2,1)}, ...), branch_computations={%region_0.0_spmd, %region_1.0_spmd} | conditional | bytes 8 | solution.py:410
  12.5 250.1 %moe_rows_176.1 = bf16[2,256,1024]{2,1,0:T(8,128)(2,1)} custom-call(bf16[2,256,1024]{2,1,0:T(8,128)(2,1)} %get-tuple-element.66.tok_ref, s32[2,2,4,256]{3,2,1,0:T(4,128)S(1)} %get-tuple-element.44.meta_ref, s32[2,2,4,8,256]{4,3,2,1,0:T(8,128)} %get-tuple-element.45.prow_ref, f32[2,2,2,256]{3,2,1,0:T(2,128)} %get-tuple-element.46.gate_ref, ...), custom_call_target="tpu_custom_call" | custom-call | tf_op jit(solution)/shard_map/cond/branch_1_fun/moe_rows_176/pallas_call | solution.py:377
  262.6 2.3 copy.20

commit v4 on v3

--- a/solution.py
+++ b/solution.py
@@ -11,6 +11,7 @@
 MESH_AXES = ("ez", "ey", "ex")
 NZ, NC, CAP = 4, 8, 32
 EXPERTS, SLOTS = NZ * NC, NC * CAP
+PACKED_ROWS = 176
 TILE = 256
 BF16, F32 = jnp.bfloat16, jnp.float32
 MESH = pl.DeviceIdType.MESH
@@ -51,47 +52,19 @@
     return {"ey": c // 4, "ex": c % 4}
 
 
-def route_kernel(ids_ref, meta_ref, prow_ref, peak_ref, mine, seen, s_sem, r_sem):
+def plan_rows(ids_ref, meta_ref, mine):
     n_layers, n_mb, top_k, n_tok = ids_ref.shape
     n_set = n_layers * n_mb
     lanes = n_set * EXPERTS
-    me_z, me_c = place()
-    me = me_z * NC + me_c
-    n_dev = NZ * NC
-
-    def target(d):
-        dev = (me + d) % n_dev
-        return {"ez": dev // NC, "ey": dev % NC // 4, "ex": dev % 4}
-
-    barrier = pltpu.get_barrier_semaphore()
-
-    def greet(d, _):
-        pl.semaphore_signal(barrier, inc=1, device_id=target(d), device_id_type=MESH)
-        return 0
-
-    lax.fori_loop(1, n_dev, greet, 0)
-
     expert = iota((EXPERTS, n_tok), 0)
     chosen = [jnp.concatenate([jnp.where(ids_ref[i // n_mb, i % n_mb, j:j + 1, :] == expert, 1.0, 0.0)
                                for i in range(n_set)], axis=0) for j in range(top_k)]
     per_tok = (chosen[0] + chosen[1]).astype(BF16)
-    counts = dot_nt(jnp.ones((8, n_tok), BF16), per_tok)
-    mine[...] = counts
-    seen[me] = counts
-    pl.semaphore_wait(barrier, n_dev - 1)
-
-    def share(d, _):
-        pltpu.make_async_remote_copy(src_ref=mine, dst_ref=seen.at[me], send_sem=s_sem, recv_sem=r_sem,
-                                     device_id=target(d), device_id_type=MESH).start()
-        return 0
-
-    lax.fori_loop(1, n_dev, share, 0)
-
+    mine[...] = dot_nt(jnp.ones((8, n_tok), BF16), per_tok)
     rank = dot(per_tok, one_hot(iota((n_tok, n_tok), 0) < iota((n_tok, n_tok), 1)))
     totals = dot(per_tok, jnp.ones((n_tok, n_tok), BF16)).astype(BF16)
     row, col = iota((lanes, lanes), 0), iota((lanes, lanes), 1)
-    same_plane = row // NC == col // NC
-    start = dot(one_hot(same_plane & (col < row)), totals)
+    start = dot(one_hot((row // NC == col // NC) & (col < row)), totals)
     which = iota((lanes, n_tok), 0) % EXPERTS
     base = which // NC * SLOTS
     packed = base.astype(F32) + rank + start
@@ -103,27 +76,26 @@
                 found = jnp.sum(chosen[j][part] * place_of[part], axis=0, keepdims=True)
                 meta_ref[i // n_mb, i % n_mb, at:at + 1, :] = found.astype(jnp.int32)
 
-    rest = pltpu.make_async_remote_copy(
-        src_ref=seen.at[pl.ds(0, n_dev - 1)], dst_ref=seen.at[pl.ds(0, n_dev - 1)], send_sem=s_sem, recv_sem=r_sem,
-        device_id=target(1), device_id_type=MESH)
-    rest.wait_recv()
+
+def plan_sources(me_z, me_c, seen, prow_ref, peak_ref):
+    n_dev, _, lanes = seen.shape
+    n_layers, n_mb = prow_ref.shape[:2]
+    row, col = iota((lanes, lanes), 0), iota((lanes, lanes), 1)
     everyone = seen[...].reshape(n_dev * 8, lanes).astype(BF16)
-    loads = dot(everyone, one_hot(same_plane))
-    peak_ref[0] = jnp.max(loads)
+    peak_ref[0] = jnp.max(dot(everyone, one_hot(row // NC == col // NC)))
     sources = jnp.concatenate([seen[source_of(me_z, k) * NC + me_c] for k in range(NZ)], axis=0).astype(BF16)
     lane_of, slot_of = iota((lanes, SLOTS), 0), iota((lanes, SLOTS), 1)
     within = iota((NZ * 8, SLOTS), 1) % CAP
-    for i in range(n_set):
+    for i in range(n_layers * n_mb):
         own = lane_of - (i * EXPERTS + me_z * NC)
         amount = dot(sources, one_hot(own == slot_of // CAP)).astype(jnp.int32)
         ahead = dot(sources, one_hot((own >= 0) & (own < slot_of // CAP))).astype(jnp.int32)
         prow_ref[i // n_mb, i % n_mb] = jnp.where(within < amount, ahead + within, -1).reshape(NZ, 8, SLOTS)
-    rest.wait_send()
-
-
-def moe_kernel(rows, tok_ref, meta_ref, prow_ref, gate_ref, w1_hbm, w3_hbm, wd_hbm, out_ref,
-               ucur, gcol, pmeta, tsend, trecv, tfull, ssend, xrecv, osend, rrecv, ysend, yrecv, w1, w3, wd, hid,
-               w_sem, m_s, m_r, tz_s, tz_r, tf_s, tf_r, sp_s, sp_r, op_s, op_r, yz_s, yz_r):
+
+
+def moe_kernel(rows, tok_ref, ids_ref, gate_ref, w1_hbm, w3_hbm, wd_hbm, out_ref, peak_ref,
+               meta_ref, prow_ref, mine, seen, ucur, gcol, pmeta, tsend, trecv, tfull, ssend, xrecv, osend, rrecv, ysend, yrecv, w1, w3, wd, hid,
+               c_s, c_r, w_sem, m_s, m_r, tz_s, tz_r, tf_s, tf_r, sp_s, sp_r, op_s, op_r, yz_s, yz_r):
     n_layers, n_mb = meta_ref.shape[0], meta_ref.shape[1]
     n_tok, width = ucur.shape[1:]
     ffn = w1.shape[-1]
@@ -278,22 +250,49 @@
             plane_all(ssend, xrecv, sp_s, sp_r, mb, k).wait_send()
             plane_all(osend, rrecv, op_s, op_r, mb, k).wait_send()
 
+    n_dev = NZ * NC
+    me = me_z * NC + me_c
+
+    def other(d):
+        dev = (me + d) % n_dev
+        return {"ez": dev // NC, "ey": dev % NC // 4, "ex": dev % 4}
+
+    def count_copy(d):
+        return pltpu.make_async_remote_copy(src_ref=mine, dst_ref=seen.at[me], send_sem=c_s, recv_sem=c_r,
+                                            device_id=other(d), device_id_type=MESH)
+
     barrier = pltpu.get_barrier_semaphore()
-    for k in range(1, NZ):
-        pl.semaphore_signal(barrier, inc=1, device_id={"ez": source(k)}, device_id_type=MESH)
-    for d in range(1, NC):
-        pl.semaphore_signal(barrier, inc=1, device_id=plane_id(peer_c(d)), device_id_type=MESH)
+
+    def greet(d, _):
+        pl.semaphore_signal(barrier, inc=1, device_id=other(d), device_id_type=MESH)
+        return 0
+
+    def share(d, _):
+        count_copy(d).start()
+        return 0
+
+    lax.fori_loop(1, n_dev, greet, 0)
     for copy in w_copies(0):
         copy.start()
     ucur[...] = tok_ref[...]
+    plan_rows(ids_ref, meta_ref, mine)
+    seen[me] = mine[...]
+    pl.semaphore_wait(barrier, n_dev - 1)
+    lax.fori_loop(1, n_dev, share, 0)
+    meta_copy(my_far).start()
+    for mb in range(n_mb):
+        send_tokens(0, mb)
+        expand_own(0, mb)
     n_gate = 2 * n_mb
     turned = jnp.transpose(gate_ref[...].reshape(n_layers * n_gate, n_tok))
     for layer in range(n_layers):
         gcol[layer] = turned[:, layer * n_gate:(layer + 1) * n_gate]
-    pl.semaphore_wait(barrier, NZ - 1 + NC - 1)
-    meta_copy(my_far).start()
-    for mb in range(n_mb):
-        send_tokens(0, mb)
+    rest = pltpu.make_async_remote_copy(
+        src_ref=seen.at[pl.ds(0, n_dev - 1)], dst_ref=seen.at[pl.ds(0, n_dev - 1)], send_sem=c_s, recv_sem=c_r,
+        device_id=other(1), device_id_type=MESH)
+    rest.wait_recv()
+    plan_sources(me_z, me_c, seen, prow_ref, peak_ref)
+    rest.wait_send()
 
     @pl.when(inner == 1)
     def _():
@@ -307,8 +306,6 @@
         return later * ((j + 1) // 3 - 1) + (1 - later) * j, later * (1 + (j + 1) % 3)
 
     def layer_step(layer, _):
-        for mb in range(n_mb):
-            expand_own(layer, mb)
         for copy in w_copies(layer):
             copy.wait()
 
@@ -338,6 +335,7 @@
             @pl.when(layer + 1 < n_layers)
             def _():
                 send_tokens(layer + 1, mb)
+                expand_own(layer + 1, mb)
         return 0
 
     lax.fori_loop(0, n_layers, layer_step, 0)
@@ -348,25 +346,11 @@
 VMEM_SPEC = pl.BlockSpec(memory_space=pltpu.VMEM)
 
 
-def run_route(ids):
-    n_layers, n_mb, top_k, n_tok = ids.shape
+def run_moe(rows, collective_id, tokens, ids, gates, w_up1, w_up3, w_down):
+    n_mb, n_tok, width = tokens.shape
+    n_layers = ids.shape[0]
     lanes = n_layers * n_mb * EXPERTS
-    return pl.pallas_call(
-        route_kernel,
-        out_shape=(jax.ShapeDtypeStruct((n_layers, n_mb, 2 * top_k, n_tok), jnp.int32),
-                   jax.ShapeDtypeStruct((n_layers, n_mb, NZ, 8, SLOTS), jnp.int32),
-                   jax.ShapeDtypeStruct((1,), F32)),
-        in_specs=[VMEM_SPEC],
-        out_specs=(VMEM_SPEC, VMEM_SPEC, pl.BlockSpec(memory_space=pltpu.SMEM)),
-        scratch_shapes=[pltpu.VMEM((8, lanes), F32), pltpu.VMEM((NZ * NC, 8, lanes), F32),
-                        pltpu.SemaphoreType.DMA, pltpu.SemaphoreType.DMA],
-        compiler_params=pltpu.CompilerParams(collective_id=0, has_side_effects=True),
-        name="route",
-    )(ids)
-
-
-def run_moe(rows, collective_id, tokens, meta, prow, gates, w_up1, w_up3, w_down):
-    n_mb, n_tok, width = tokens.shape
+    meta = (n_layers, n_mb, 4, n_tok)
     ffn = w_up1.shape[-1]
     hbm = pl.BlockSpec(memory_space=pl.ANY)
     per_mb = pltpu.VMEM((n_mb, n_tok, width), BF16)
@@ -376,15 +360,18 @@
     pair = pltpu.SemaphoreType.DMA((n_mb, NZ))
     return pl.pallas_call(
         functools.partial(moe_kernel, rows),
-        out_shape=jax.ShapeDtypeStruct(tokens.shape, BF16),
-        in_specs=[VMEM_SPEC] * 4 + [hbm] * 3,
-        out_specs=VMEM_SPEC,
+        out_shape=(jax.ShapeDtypeStruct(tokens.shape, BF16), jax.ShapeDtypeStruct((1,), F32)),
+        in_specs=[VMEM_SPEC] * 3 + [hbm] * 3,
+        out_specs=(VMEM_SPEC, pl.BlockSpec(memory_space=pltpu.SMEM)),
         scratch_shapes=[
-            per_mb, pltpu.VMEM((meta.shape[0], n_tok, 2 * n_mb), F32), pltpu.VMEM((2,) + meta.shape, jnp.int32),
+            pltpu.VMEM(meta, jnp.int32), pltpu.VMEM((n_layers, n_mb, NZ, 8, SLOTS), jnp.int32),
+            pltpu.VMEM((8, lanes), F32), pltpu.VMEM((EXPERTS, 8, lanes), F32),
+            per_mb, pltpu.VMEM((n_layers, n_tok, 2 * n_mb), F32), pltpu.VMEM((2,) + meta, jnp.int32),
             relay, relay, pltpu.VMEM((n_mb, 2, n_tok, width), BF16),
             padded, padded, padded, padded, packed, packed,
             pltpu.VMEM((width, ffn), BF16), pltpu.VMEM((width, ffn), BF16), pltpu.VMEM((ffn, width), BF16),
             pltpu.VMEM((SLOTS, ffn), BF16),
+            pltpu.SemaphoreType.DMA, pltpu.SemaphoreType.DMA,
             pltpu.SemaphoreType.DMA((3,)), pltpu.SemaphoreType.DMA((1,)), pltpu.SemaphoreType.DMA((2,)),
             pltpu.SemaphoreType.DMA((n_mb, 3)), pltpu.SemaphoreType.DMA((n_mb, 3)),
             pltpu.SemaphoreType.DMA((n_mb,)), pltpu.SemaphoreType.DMA((n_mb, 2)),
@@ -392,7 +379,7 @@
         compiler_params=pltpu.CompilerParams(
             collective_id=collective_id, has_side_effects=True, vmem_limit_bytes=67_000_000),
         name=f"moe_rows_{rows}",
-    )(tokens, meta, prow, gates, w_up1, w_up3, w_down)
+    )(tokens, ids, gates, w_up1, w_up3, w_down)
 
 
 def solution(mesh):
@@ -401,12 +388,10 @@
     weight_spec = P(None, MESH_AXES, None, None)
 
     def device_body(tokens_in, expert_ids, gate_vals, w_up1, w_up3, w_down):
-        meta, prow, peak = run_route(expert_ids.transpose(0, 1, 3, 2))
+        ids = expert_ids.transpose(0, 1, 3, 2)
         gates = gate_vals.transpose(0, 1, 3, 2)
-
-        def branch(rows, collective_id):
-            return lambda: run_moe(rows, collective_id, tokens_in, meta, prow, gates, w_up1, w_up3, w_down)
-
-        return lax.cond(peak[0] <= 176.0, branch(176, 1), branch(SLOTS, 2))
+        args = (tokens_in, ids, gates, w_up1, w_up3, w_down)
+        out, peak = run_moe(PACKED_ROWS, 1, *args)
+        return lax.cond(peak[0] <= PACKED_ROWS, lambda: out, lambda: run_moe(SLOTS, 2, *args)[0])
 
     return jax.shard_map(device_body, mesh=mesh, in_specs=(tok_spec, route_spec, route_spec, weight_spec, weight_spec, weight_spec), out_specs=tok_spec, check_vma=False)

time: 265 us -> 252 us (0.951)
  Pallas kernels: 262 us -> 249 us
    pallas_call x2 -> x1, Pallas kernels: 262 us -> 249 us  [run_moe(): pl.pallas_call(functools.partial(moe_kernel, rows), out_shape=(jax.ShapeD...]
where the time goes in v4:
time: 252 us
  Pallas kernels  249 us (99%)
    pallas_call x1, Pallas kernels, run_moe(): pl.pallas_call(functools.partial(moe_kernel, rows), out_shape=(jax.ShapeD...  249 us

profile of v4, /device:TPU:0, one launch (start us, length us, event | category | flops | bytes accessed | tf_op | source)
XLA Modules:
  0.0 252.0 jit_solution(1165436524906155665)
XLA Ops:
  0.0 0.0 copy-start
  0.0 0.0 copy-start.1
  0.0 248.9 %moe_rows_176.1 = (bf16[2,256,1024]{2,1,0:T(8,128)(2,1)}, f32[1]{0:T(128)}) custom-call(bf16[2,256,1024]{2,1,0:T(8,128)(2,1)} %tok_ref.1, s32[2,2,2,256]{3,2,1,0:T(2,128)} %bitcast.3, f32[2,2,2,256]{3,2,1,0:T(2,128)} %bitcast.5, bf16[2,1,1024,2816]{3,2,1,0:T(8,128)(2,1)} %w1_hbm.1, bf16[2,1,1024,2816]{3,2,1,0:T(8,128)(2,1)} %w3_hbm.1, ...), custom_call_target="tpu_custom_call" | custom-call | tf_op jit(solution)/shard_map/moe_rows_176/pallas_call | solution.py:361
  249.5 0.0 copy-done
  249.5 0.0 copy-done.1
  249.5 0.2 conditional.1
  249.7 2.3 copy.12
Async XLA Ops:
  0.0 249.5 %copy-start = (s32[2,2,256,2]{2,3,1,0:T(2,128)S(1)}, s32[2,2,256,2]{2,3,1,0:T(2,128)}, u32[]{:S(2)}) copy-start(s32[2,2,256,2]{2,3,1,0:T(2,128)} %param.9) | copy-start | bytes 24580
  0.0 249.5 %copy-start.1 = (f32[2,2,256,2]{2,3,1,0:T(2,128)S(1)}, f32[2,2,256,2]{2,3,1,0:T(2,128)}, u32[]{:S(2)}) copy-start(f32[2,2,256,2]{2,3,1,0:T(2,128)} %param.10) | copy-start | bytes 24580

commit v5 on v4

--- a/solution.py
+++ b/solution.py
@@ -12,6 +12,7 @@
 NZ, NC, CAP = 4, 8, 32
 EXPERTS, SLOTS = NZ * NC, NC * CAP
 PACKED_ROWS = 176
+PLANE_ORDER = (6, 7, 2, 4, 3, 5, 1)
 TILE = 256
 BF16, F32 = jnp.bfloat16, jnp.float32
 MESH = pl.DeviceIdType.MESH
@@ -107,7 +108,7 @@
     my_far = 1 - inner
 
     def peer_c(d):
-        return (me_c + d) % NC
+        return sum(bit * ((me_c // bit + d // bit) % 2) for bit in (1, 2, 4))
 
     def w_copies(layer):
         return [pltpu.make_async_copy(src.at[layer, 0], dst, w_sem.at[i])
@@ -165,7 +166,7 @@
 
     def spread(mb, k, block):
         ssend[mb, k] = block.astype(BF16).reshape(NC, CAP, width)
-        for d in range(1, NC):
+        for d in PLANE_ORDER:
             plane_copy(ssend, xrecv, sp_s, sp_r, mb, k, d).start()
         xrecv[mb, k, me_c] = ssend[mb, k, me_c]
 
@@ -208,7 +209,7 @@
             return 0
 
         lax.fori_loop(0, width // TILE, down, 0, unroll=True)
-        for d in range(1, NC):
+        for d in PLANE_ORDER:
             plane_copy(osend, rrecv, op_s, op_r, mb, k, d).start()
         rrecv[mb, k, me_c] = osend[mb, k, me_c]
 

time: 252 us -> 252 us (level)
  no operation moved by 1% of the time
where the time goes in v5:
time: 252 us; the launch traced here: 251 us
  Pallas kernels  248 us (98%)
    pallas_call x1, Pallas kernels, run_moe(): pl.pallas_call(functools.partial(moe_kernel, rows), out_shape=(jax.ShapeD...  248 us

profile of v5, /device:TPU:0, one launch (start us, length us, event | category | flops | bytes accessed | tf_op | source)
XLA Modules:
  0.0 251.3 jit_solution(5090709110850637919)
XLA Ops:
  0.0 0.0 copy-start
  0.0 0.0 copy-start.1
  0.0 248.2 %moe_rows_176.1 = (bf16[2,256,1024]{2,1,0:T(8,128)(2,1)}, f32[1]{0:T(128)}) custom-call(bf16[2,256,1024]{2,1,0:T(8,128)(2,1)} %tok_ref.1, s32[2,2,2,256]{3,2,1,0:T(2,128)} %bitcast.3, f32[2,2,2,256]{3,2,1,0:T(2,128)} %bitcast.5, bf16[2,1,1024,2816]{3,2,1,0:T(8,128)(2,1)} %w1_hbm.1, bf16[2,1,1024,2816]{3,2,1,0:T(8,128)(2,1)} %w3_hbm.1, ...), custom_call_target="tpu_custom_call" | custom-call | tf_op jit(solution)/shard_map/moe_rows_176/pallas_call | solution.py:362
  248.9 0.0 copy-done
  248.9 0.0 copy-done.1
  248.9 0.2 conditional.1
  249.1 2.3 copy.12
Async XLA Ops:
  0.0 248.9 %copy-start = (s32[2,2,256,2]{2,3,1,0:T(2,128)S(1)}, s32[2,2,256,2]{2,3,1,0:T(2,128)}, u32[]{:S(2)}) copy-start(s32[2,2,256,2]{2,3,1,0:T(2,128)} %param.9) | copy-start | bytes 24580
  0.0 248.9 %copy-start.1 = (f32[2,2,256,2]{2,3,1,0:T(2,128)S(1)}, f32[2,2,256,2]{2,3,1,0:T(2,128)}, u32[]{:S(2)}) copy-start(f32[2,2,256,2]{2,3,1,0:T(2,128)} %param.10) | copy-start | bytes 24580
